TPU v7x, 32 devices: a whole 2x2x4 slice. The times are simulated.
32 devices in a mesh: grp: 2 (over x), path: 8 (over z, y), amp: 2 (over core).
Axes of the slice: x: 2, y: 2, z: 4, core: 2. Of those that a mesh axis runs over, the one named last changes fastest.
Arguments:
- left_slabs: bfloat16 [256, 2, 16384], P(('grp', 'path'), None, 'amp'), parts along dimension 0, may hold values from -0.59765625 to 0.59765625
- right_slabs: bfloat16 [256, 2, 8192], P(('grp', 'path'), None, 'amp'), parts along dimension 0, may hold values from -0.59765625 to 0.59765625
- term_index: int32 [256], P(('grp', 'path')), parts along dimension 0, may hold values from 0 to 3
- left_terms: float32 [4, 2, 2, 2], replicated, may hold values from -4.2 to 4.2
- right_terms: float32 [4, 2, 2, 2], replicated, may hold values from -4.2 to 4.2
- left_gates: bfloat16 [2, 2, 128, 128], replicated, may hold values from -0.375 to 0.375
- right_gates: bfloat16 [2, 2, 128, 128], replicated, may hold values from -0.375 to 0.375
Outputs:
- amplitudes: bfloat16 [2, 32768, 8192], P(None, ('grp', 'path'), 'amp'), parts along dimension 1
There are 2 independent parts, one for each index of `grp`. A program takes and returns all parts, laid end to end along the dimension named above; an argument that names none is the same for every part. Nothing has to cross between parts.
All inputs are finite; a program needn't handle non-finite values.
Results may differ from a plain program's by a relative error of at most 0.0081.
Values may be sent and summed in bfloat16 or wider, within the bound.
No kernel may reach another device: no remote copies, remote signals or barrier semaphores. Data moves between devices by JAX's collectives and lax.ppermute only.
A program may use at most 128 MiB of HBM per device.

v0:
```python
import jax
import jax.numpy as jnp
from jax import lax
from jax.experimental import pallas as pl
from jax.experimental.pallas import tpu as pltpu
from jax.sharding import PartitionSpec as P


F32 = jnp.float32
BF16 = jnp.bfloat16


def iota(shape, dim):
    return lax.broadcasted_iota(jnp.int32, shape, dim)


def one_hot(test):
    return jnp.where(test, 1.0, 0.0).astype(BF16)


def dot(a, b):
    return jnp.dot(a, b, preferred_element_type=F32)


def swap_pairs(x, axis):
    size = x.shape[axis]
    even = iota(x.shape, axis) % 2 == 0
    return jnp.where(even, pltpu.roll(x, size - 1, axis), pltpu.roll(x, 1, axis))


def swap_rows(x):
    rows, width = x.shape
    return swap_pairs(x.reshape(rows // 8, 8, width), 1).reshape(rows, width)


def row_sign(shape):
    return jnp.where(iota(shape, 0) % 2 == 0, -1.0, 1.0).astype(F32)


def stacked_gate(gates_ref, select, place):
    gate_width = gates_ref.shape[-1]
    columns = iota((gate_width, 2 * gate_width), 1)
    real_at = one_hot(columns == place)
    imag_at = one_hot(columns == place + 1)
    real = dot(select, gates_ref[1, 0]).astype(BF16)
    imag = dot(select, gates_ref[1, 1]).astype(BF16)
    top = dot(real, real_at) - dot(imag, imag_at)
    bottom = dot(imag, real_at) + dot(real, imag_at)
    return jnp.concatenate([top, bottom], 0).astype(BF16)


def cut_and_low(rows, path, index_ref, terms_ref, gates_ref):
    width = rows.shape[1]
    term = index_ref[path]
    parity = iota((1, width), 1) % 2 == 0

    def pattern(part, first, second):
        return jnp.where(parity, terms_ref[part, 0, first, term], terms_ref[part, 1, second, term])

    sign = row_sign(rows.shape)
    value = rows.astype(F32)
    turned = swap_rows(value) * sign
    cut = (
        value * pattern(0, 0, 1)
        + turned * pattern(1, 0, 1)
        + swap_pairs(value, 1) * pattern(0, 1, 0)
        + swap_pairs(turned, 1) * pattern(1, 1, 0)
    ).astype(BF16)
    gate = gates_ref[0].reshape(2 * width, width)
    low = lax.dot_general(cut, gate, (((1,), (1,)), ((), ())), preferred_element_type=F32)
    return (low[:, :width] + swap_rows(low[:, width:]) * sign).astype(BF16)


def left_kernel(count, index_ref, terms_ref, gates_ref, own_ref, other_ref, *rest):
    out_refs, stage = rest[:count], rest[count]
    paths, _, width = own_ref.shape
    mine, core = lax.axis_index("path"), lax.axis_index("amp")
    half = width // 2
    part = half // count
    which = iota((half, width), 0)
    target = ((which // part) ^ mine) * (2 * part) + core * part + which % part
    select = one_hot(iota((half, width), 1) == target)
    source = iota((width, 2 * width), 0)
    place = ((source // half) ^ core) * width + (source % half) * 2
    matrix = stacked_gate(gates_ref, select, place)
    slots = 2 * paths

    for pair in range(0, paths, 2):
        columns = []
        for path in (pair, pair + 1):
            parts = [
                cut_and_low(ref[path], path, index_ref, terms_ref, gates_ref)
                for ref in (own_ref, other_ref)
            ]
            columns.append(jnp.concatenate(parts, 0))
        turned = dot(matrix, jnp.concatenate(columns, 1))
        for at, path in enumerate((pair, pair + 1)):
            for ri in range(2):
                stage[pl.ds(ri * paths + path, half, stride=slots), :] = turned[
                    ri * half : (ri + 1) * half, at * width : (at + 1) * width
                ]
    for k in range(count):
        rows = stage[k * part * slots : (k + 1) * part * slots, :]
        out_refs[k][...] = rows.astype(BF16).reshape(part, slots, width)


def right_kernel(index_ref, terms_ref, gates_ref, own_ref, other_ref, out_ref, stage):
    paths, _, width = own_ref.shape
    core = lax.axis_index("amp")
    half, quarter = width // 2, width // 4
    which = iota((half, width), 0)
    target = 2 * (core * quarter + which % quarter) + which // quarter
    select = one_hot(iota((half, width), 1) == target)
    source = iota((width, 2 * width), 0)
    group = source // 2
    place = (source % 2) * width + ((group // quarter) ^ core) * half + (group % quarter) * 2
    matrix = stacked_gate(gates_ref, select, place)
    slots = 2 * paths
    front = iota((1, width), 1) < half

    for four in range(0, paths, 4):
        columns = []
        for pair in (four, four + 2):
            first, second = [
                jnp.concatenate(
                    [
                        cut_and_low(ref[path], path, index_ref, terms_ref, gates_ref)
                        for ref in (own_ref, other_ref)
                    ],
                    0,
                ).astype(F32)
                for path in (pair, pair + 1)
            ]
            upper = jnp.where(front, first, pltpu.roll(second, half, 1))
            lower = jnp.where(front, pltpu.roll(first, half, 1), second)
            columns.append(jnp.concatenate([upper, lower], 0).astype(BF16))
        turned = dot(matrix, jnp.concatenate(columns, 1))
        for at, pair in enumerate((four, four + 2)):
            for ri in range(2):
                block = turned[ri * half : (ri + 1) * half, at * width : (at + 1) * width]
                upper, lower = block[:quarter], block[quarter:]
                stage[pl.ds(ri * paths + pair, quarter, stride=slots), :] = jnp.where(
                    front, upper, pltpu.roll(lower, half, 1)
                )
                stage[pl.ds(ri * paths + pair + 1, quarter, stride=slots), :] = jnp.where(
                    front, pltpu.roll(upper, half, 1), lower
                )
    out_ref[...] = stage[...].astype(BF16).reshape(out_ref.shape)


def arrange_kernel(count, *refs):
    pieces, out_ref = refs[:count], refs[count]
    part, slots, width = pieces[0].shape
    paths = slots // 2
    for j in range(part):
        plain, crossed = [], []
        for piece in pieces:
            block = piece[j].astype(F32)
            real, imag = block[:paths], block[paths:]
            plain += [real, -imag]
            crossed += [imag, real]
        for at, rows in enumerate((plain, crossed)):
            out_ref[at, j * width : (j + 1) * width, :] = jnp.concatenate(rows, 0).T.astype(BF16)


def contract_kernel(count, step, own_ref, other_ref, *refs):
    pieces, out_ref = refs[:count], refs[count]
    left, right, staged, in_sems, out_sems = refs[count + 1 :]
    core = lax.axis_index("amp")
    rows = own_ref.shape[1]
    groups, slots, width = pieces[0].shape
    span = step * width
    copies = [
        pltpu.make_async_copy(
            ref, left.at[:, pl.ds(pl.multiple_of(where * rows, rows), rows), :], in_sems.at[at]
        )
        for at, (ref, where) in enumerate(((own_ref, core), (other_ref, 1 - core)))
    ] + [
        pltpu.make_async_copy(piece, right.at[:, pl.ds(k * slots, slots), :], in_sems.at[2 + k])
        for k, piece in enumerate(pieces)
    ]
    for copy in copies:
        copy.start()
    for copy in copies:
        copy.wait()
    buffers = staged.shape[0]

    def write(i, slot):
        place = pl.ds(pl.multiple_of(i * span, span), span)
        return pltpu.make_async_copy(staged.at[slot], out_ref.at[:, :, place], out_sems.at[slot])

    tile = min(256, 2 * rows)

    @pl.loop(0, groups // step)
    def _(i):
        slot = lax.rem(i, buffers)

        @pl.when(i >= buffers)
        def _():
            write(i - buffers, slot).wait()

        block = jnp.concatenate([right[i * step + g] for g in range(step)], 1)
        for part in range(2):
            for start in range(0, 2 * rows, tile):
                staged[slot, part, start : start + tile, :] = dot(
                    left[part, start : start + tile, :], block
                ).astype(BF16)
        write(i, slot).start()

    for i in range(groups // step - buffers, groups // step):
        write(i, i % buffers).wait()


SMEM = pl.BlockSpec(memory_space=pltpu.SMEM)
VMEM = pl.BlockSpec(memory_space=pltpu.VMEM)
ANY = pl.BlockSpec(memory_space=pl.ANY)


def as_rows(slab, width):
    paths, _, length = slab.shape
    groups = length // width
    return slab.reshape(paths, 2, groups, width).transpose(0, 2, 1, 3).reshape(paths, 2 * groups, width)


def shards(left_slabs, right_slabs, term_index, left_terms, right_terms, left_gates, right_gates):
    width = left_gates.shape[-1]
    count = lax.axis_size("path")
    paths = left_slabs.shape[0]
    slots = 2 * paths

    def swap(x):
        return lax.ppermute(x, "amp", [(0, 1), (1, 0)])

    def hop(x, k):
        return lax.ppermute(x, "path", [(i, i ^ k) for i in range(count)])

    right_other = swap(right_slabs)
    left_other = swap(left_slabs)

    groups = right_slabs.shape[2] // width
    right = pl.pallas_call(
        right_kernel,
        in_specs=[SMEM, SMEM, VMEM, VMEM, VMEM],
        out_specs=VMEM,
        out_shape=jax.ShapeDtypeStruct((groups, slots, width), BF16),
        scratch_shapes=[pltpu.VMEM((groups * slots, width), F32)],
        cost_estimate=pl.CostEstimate(flops=2 * 10**9, bytes_accessed=10**6, transcendentals=0),
        compiler_params=pltpu.CompilerParams(vmem_limit_bytes=24 * 2**20),
        name="right_prep",
    )(
        term_index,
        right_terms.transpose(1, 2, 3, 0),
        right_gates,
        as_rows(right_slabs, width),
        as_rows(right_other, width),
    )

    part = width // 2 // count
    left = pl.pallas_call(
        lambda *refs: left_kernel(count, *refs),
        in_specs=[SMEM, SMEM, VMEM, VMEM, VMEM],
        out_specs=[VMEM] * count,
        out_shape=[jax.ShapeDtypeStruct((part, slots, width), BF16)] * count,
        scratch_shapes=[pltpu.VMEM((width // 2 * slots, width), F32)],
        cost_estimate=pl.CostEstimate(flops=4 * 10**9, bytes_accessed=2 * 10**6, transcendentals=0),
        compiler_params=pltpu.CompilerParams(vmem_limit_bytes=24 * 2**20),
        name="left_prep",
    )(term_index, left_terms.transpose(1, 2, 3, 0), left_gates, as_rows(left_slabs, width), as_rows(left_other, width))

    pieces = {0: right}
    bit = count // 2
    while bit:
        for k in sorted(pieces):
            pieces[k | bit] = hop(pieces[k], bit)
        bit //= 2

    pairs = [jnp.concatenate([left[k + 1] for k in range(0, count, 2)], 0)]
    if count > 1:
        pairs = [hop(pairs[0], 1)]
    blocks = {}
    for k in range(0, count, 2):
        both = jnp.concatenate([left[k], pairs[0][k // 2 * part : (k // 2 + 1) * part]], 0)
        if k:
            both = hop(both, k)
        blocks[k], blocks[k + 1] = both[:part], both[part:]
    blocks = [blocks[k] for k in range(count)]
    rows = part * width
    own = pl.pallas_call(
        lambda *refs: arrange_kernel(count, *refs),
        in_specs=[VMEM] * count,
        out_specs=VMEM,
        out_shape=jax.ShapeDtypeStruct((2, rows, count * slots), BF16),
        cost_estimate=pl.CostEstimate(flops=2 * 10**9, bytes_accessed=10**6, transcendentals=0),
        compiler_params=pltpu.CompilerParams(vmem_limit_bytes=16 * 2**20),
        name="left_arrange",
    )(*blocks)
    other = swap(own)

    step = 4
    return pl.pallas_call(
        lambda *refs: contract_kernel(count, step, *refs),
        in_specs=[ANY] * (2 + count),
        out_specs=ANY,
        out_shape=jax.ShapeDtypeStruct((2, 2 * rows, groups * width), BF16),
        scratch_shapes=[
            pltpu.VMEM((2, 2 * rows, count * slots), BF16),
            pltpu.VMEM((groups, count * slots, width), BF16),
            pltpu.VMEM((4, 2, 2 * rows, step * width), BF16),
            pltpu.SemaphoreType.DMA((2 + count,)),
            pltpu.SemaphoreType.DMA((4,)),
        ],
        cost_estimate=pl.CostEstimate(flops=9 * 10**9, bytes_accessed=36 * 10**6, transcendentals=0),
        compiler_params=pltpu.CompilerParams(vmem_limit_bytes=40 * 2**20),
        name="contract",
    )(own, other, *[pieces[k] for k in range(count)])


def solution(mesh):
    return jax.shard_map(
        shards,
        mesh=mesh,
        in_specs=(
            P(("grp", "path"), None, "amp"),
            P(("grp", "path"), None, "amp"),
            P(("grp", "path")),
            P(),
            P(),
            P(),
            P(),
        ),
        out_specs=P(None, ("grp", "path"), "amp"),
        check_vma=False,
    )
```

profile of v0, /device:TPU:0, one launch (start us, length us, event | category | flops | bytes accessed | tf_op | source)
XLA Modules:
  0.0 91.9 jit_solution(8028138643264966007)
XLA Ops:
  0.0 0.5 collective-permute-start
  0.5 1.7 %collective-permute-done = bf16[16,2,8192]{2,1,0:T(2,128)(2,1)S(1)} collective-permute-done((bf16[16,2,8192]{2,1,0:T(2,128)(2,1)}, bf16[16,2,8192]{2,1,0:T(2,128)(2,1)S(1)}, u32[]{:S(2)}, u32[]{:S(2)}) %collective-permute-start) | collective-permute-done | bytes 524320 | tf_op jit(solution)/shard_map/ppermute | solution.py:232
  2.2 1.0 %copy-done = bf16[16,2,8192]{2,1,0:T(2,128)(2,1)S(1)} copy-done((bf16[16,2,8192]{2,1,0:T(2,128)(2,1)S(1)}, bf16[16,2,8192]{2,1,0:T(2,128)(2,1)}, u32[]{:S(2)}) %copy-start) | copy-done | bytes 524312
  3.3 0.9 copy-done.2
  4.2 0.7 copy-done.4
  4.9 0.7 copy-done.6
  5.5 3.4 %left_prep.1 = (bf16[8,32,128]{2,1,0:T(8,128)(2,1)S(1)}, bf16[8,32,128]{2,1,0:T(8,128)(2,1)S(1)}, bf16[8,32,128]{2,1,0:T(8,128)(2,1)S(1)}, bf16[8,32,128]{2,1,0:...) custom-call(s32[16]{0:T(128)S(1)} %copy-done.6, ...), custom_call_target="tpu_custom_call" | custom-call | flops 4000000000 | bytes 2000000 | tf_op jit(solution)/shard_map/left_prep/pallas_call | solution.py:259
  8.9 2.9 %collective-permute-start.1 = (bf16[32,32,128]{2,1,0:T(8,128)(2,1)S(1)}, bf16[32,32,128]{2,1,0:T(8,128)(2,1)S(1)}, u32[]{:S(2)}, u32[]{:S(2)}) collective-permute-start(bf16[32,32,128]{2,1,0:T(8,128)(2,1)S(1)} %pad_maximum_fusion), channel_id=1, source_target_pairs={{0,2},{2,0},{4,6},{6,4},{8,10},{10,8},{12,14},{14,12},{1,3},{3,1},... | collective-permute-start | bytes 786440 | tf_op jit(solution)/shard_map/ppermute | solution.py:235
  11.9 6.6 %collective-permute-done.1 = bf16[32,32,128]{2,1,0:T(8,128)(2,1)S(1)} collective-permute-done((bf16[32,32,128]{2,1,0:T(8,128)(2,1)S(1)}, bf16[32,32,128]{2,1,0:T(8,128)(2,1)S(1)}, u32[]{:S(2)}, u32[]{:S(2)}) %collective-permute-start.1) | collective-permute-done | bytes 262176 | tf_op jit(solution)/shard_map/ppermute | solution.py:235
  18.5 1.9 %collective-permute-start.2 = (bf16[16,32,128]{2,1,0:T(8,128)(2,1)S(1)}, bf16[16,32,128]{2,1,0:T(8,128)(2,1)S(1)}, u32[]{:S(2)}, u32[]{:S(2)}) collective-permute-start(bf16[16,32,128]{2,1,0:T(8,128)(2,1)S(1)} %pad_maximum_fusion.1), channel_id=1, source_target_pairs={{0,4},{2,6},{4,0},{6,2},{8,12},{10,14},{12,8},{14,10},{1,5},{3,7},... | collective-permute-start | bytes 393224 | tf_op jit(solution)/shard_map/ppermute | solution.py:235
  20.4 2.7 %collective-permute-start.3 = (bf16[16,32,128]{2,1,0:T(8,128)(2,1)S(1)}, bf16[16,32,128]{2,1,0:T(8,128)(2,1)S(1)}, u32[]{:S(2)}, u32[]{:S(2)}) collective-permute-start(bf16[16,32,128]{2,1,0:T(8,128)(2,1)S(1)} %pad_maximum_fusion.2), channel_id=1, source_target_pairs={{0,8},{2,10},{4,12},{6,14},{8,0},{10,2},{12,4},{14,6},{1,9},{3,11}... | collective-permute-start | bytes 393224 | tf_op jit(solution)/shard_map/ppermute | solution.py:235
  23.1 0.1 collective-permute-start.4
  23.2 1.8 %collective-permute-done.2 = bf16[16,32,128]{2,1,0:T(8,128)(2,1)S(1)} collective-permute-done((bf16[16,32,128]{2,1,0:T(8,128)(2,1)S(1)}, bf16[16,32,128]{2,1,0:T(8,128)(2,1)S(1)}, u32[]{:S(2)}, u32[]{:S(2)}) %collective-permute-start.2) | collective-permute-done | bytes 131104 | tf_op jit(solution)/shard_map/ppermute | solution.py:235
  25.0 7.9 %collective-permute-done.3 = bf16[16,32,128]{2,1,0:T(8,128)(2,1)S(1)} collective-permute-done((bf16[16,32,128]{2,1,0:T(8,128)(2,1)S(1)}, bf16[16,32,128]{2,1,0:T(8,128)(2,1)S(1)}, u32[]{:S(2)}, u32[]{:S(2)}) %collective-permute-start.3) | collective-permute-done | bytes 131104 | tf_op jit(solution)/shard_map/ppermute | solution.py:235
  32.9 0.3 left_arrange.1.refs_0_
  33.2 0.1 collective-permute-start.5
  33.3 0.9 %copy-done.1 = bf16[16,2,4096]{2,1,0:T(2,128)(2,1)S(1)} copy-done((bf16[16,2,4096]{2,1,0:T(2,128)(2,1)S(1)}, bf16[16,2,4096]{2,1,0:T(2,128)(2,1)}, u32[]{:S(2)}) %copy-start.1) | copy-done | bytes 262168
  34.2 0.9 copy-done.3
  35.2 0.7 copy-done.5
  35.8 2.7 %right_prep.1.refs_2_ = bf16[32,32,128]{2,1,0:T(8,128)(2,1)S(1)} custom-call(s32[16]{0:T(128)S(1)} %copy-done.6, f32[2,2,2,4]{3,2,1,0:T(2,128)S(1)} %bitcast.27, bf16[2,2,128,128]{3,2,1,0:T(8,128)(2,1)S(1)} %copy-done.3, bf16[16,64,128]{2,1,0:T(8,128)(2,1)S(1)} %bitcast.24, bf16[16,64,128]{2,1,0:T(8,128)(2,1)S(1)} %bitcast.25), custom_call_target="tpu_custom_call" | custom-call | flops 2000000000 | bytes 1000000 | tf_op jit(solution)/shard_map/right_prep/pallas_call | solution.py:241
  38.6 3.1 %collective-permute-start.10 = (bf16[32,32,128]{2,1,0:T(8,128)(2,1)S(1)}, bf16[32,32,128]{2,1,0:T(8,128)(2,1)S(1)}, u32[]{:S(2)}, u32[]{:S(2)}) collective-permute-start(bf16[32,32,128]{2,1,0:T(8,128)(2,1)S(1)} %right_prep.1.refs_2_), channel_id=1, source_target_pairs={{0,8},{2,10},{4,12},{6,14},{8,0},{10,2},{12,4},{14,6},{1,9},{3,11}... | collective-permute-start | bytes 786440 | tf_op jit(solution)/shard_map/ppermute | solution.py:235
  41.6 0.1 collective-permute-start.8
  41.7 12.6 %collective-permute-done.10.refs_6_ = bf16[32,32,128]{2,1,0:T(8,128)(2,1)S(1)} collective-permute-done((bf16[32,32,128]{2,1,0:T(8,128)(2,1)S(1)}, bf16[32,32,128]{2,1,0:T(8,128)(2,1)S(1)}, u32[]{:S(2)}, u32[]{:S(2)}) %collective-permute-start.10) | collective-permute-done | bytes 262176 | tf_op jit(solution)/shard_map/ppermute | solution.py:235
  54.3 1.5 %collective-permute-start.7 = (bf16[32,32,128]{2,1,0:T(8,128)(2,1)S(1)}, bf16[32,32,128]{2,1,0:T(8,128)(2,1)S(1)}, u32[]{:S(2)}, u32[]{:S(2)}) collective-permute-start(bf16[32,32,128]{2,1,0:T(8,128)(2,1)S(1)} %right_prep.1.refs_2_), channel_id=1, source_target_pairs={{0,2},{2,0},{4,6},{6,4},{8,10},{10,8},{12,14},{14,12},{1,3},{3,1},... | collective-permute-start | bytes 786440 | tf_op jit(solution)/shard_map/ppermute | solution.py:235
  55.8 0.5 collective-permute-start.11
  56.3 1.5 %collective-permute-start.9 = (bf16[32,32,128]{2,1,0:T(8,128)(2,1)S(1)}, bf16[32,32,128]{2,1,0:T(8,128)(2,1)S(1)}, u32[]{:S(2)}, u32[]{:S(2)}) collective-permute-start(bf16[32,32,128]{2,1,0:T(8,128)(2,1)S(1)} %collective-permute-done.8.refs_4_), channel_id=1, source_target_pairs={{0,2},{2,0},{4,6},{6,4},{8,10},{10,8},{12,14},{14,12},{1,3},{3,1},... | collective-permute-start | bytes 786440 | tf_op jit(solution)/shard_map/ppermute | solution.py:235
  57.9 4.5 %collective-permute-done.12.refs_8_ = bf16[32,32,128]{2,1,0:T(8,128)(2,1)S(1)} collective-permute-done((bf16[32,32,128]{2,1,0:T(8,128)(2,1)S(1)}, bf16[32,32,128]{2,1,0:T(8,128)(2,1)S(1)}, u32[]{:S(2)}, u32[]{:S(2)}) %collective-permute-start.12) | collective-permute-done | bytes 262176 | tf_op jit(solution)/shard_map/ppermute | solution.py:235
  62.4 1.5 %collective-permute-start.13 = (bf16[32,32,128]{2,1,0:T(8,128)(2,1)S(1)}, bf16[32,32,128]{2,1,0:T(8,128)(2,1)S(1)}, u32[]{:S(2)}, u32[]{:S(2)}) collective-permute-start(bf16[32,32,128]{2,1,0:T(8,128)(2,1)S(1)} %collective-permute-done.12.refs_8_), channel_id=1, source_target_pairs={{0,2},{2,0},{4,6},{6,4},{8,10},{10,8},{12,14},{14,12},{1,3},{3,1},... | collective-permute-start | bytes 786440 | tf_op jit(solution)/shard_map/ppermute | solution.py:235
  63.9 5.2 %collective-permute-done.11.refs_7_ = bf16[32,32,128]{2,1,0:T(8,128)(2,1)S(1)} collective-permute-done((bf16[32,32,128]{2,1,0:T(8,128)(2,1)S(1)}, bf16[32,32,128]{2,1,0:T(8,128)(2,1)S(1)}, u32[]{:S(2)}, u32[]{:S(2)}) %collective-permute-start.11) | collective-permute-done | bytes 262176 | tf_op jit(solution)/shard_map/ppermute | solution.py:235
  69.1 5.6 %collective-permute-done.9.refs_5_ = bf16[32,32,128]{2,1,0:T(8,128)(2,1)S(1)} collective-permute-done((bf16[32,32,128]{2,1,0:T(8,128)(2,1)S(1)}, bf16[32,32,128]{2,1,0:T(8,128)(2,1)S(1)}, u32[]{:S(2)}, u32[]{:S(2)}) %collective-permute-start.9) | collective-permute-done | bytes 262176 | tf_op jit(solution)/shard_map/ppermute | solution.py:235
  74.7 4.5 %collective-permute-done.13.refs_9_ = bf16[32,32,128]{2,1,0:T(8,128)(2,1)S(1)} collective-permute-done((bf16[32,32,128]{2,1,0:T(8,128)(2,1)S(1)}, bf16[32,32,128]{2,1,0:T(8,128)(2,1)S(1)}, u32[]{:S(2)}, u32[]{:S(2)}) %collective-permute-start.13) | collective-permute-done | bytes 262176 | tf_op jit(solution)/shard_map/ppermute | solution.py:235
  79.2 12.7 %contract.1 = bf16[2,2048,4096]{2,1,0:T(8,128)(2,1)} custom-call(bf16[2,1024,256]{2,1,0:T(8,128)(2,1)S(1)} %left_arrange.1.refs_0_, bf16[2,1024,256]{2,1,0:T(8,128)(2,1)S(1)} %collective-permute-done.5.refs_1_, bf16[32,32,128]{2,1,0:T(8,128)(2,1)S(1)} %right_prep.1.refs_2_, bf16[32,32,128]{2,1,0:T(8,128)(2,1)S(1)} %collective-permute-done.7.refs_3_, ...), custom_call_target="tpu_custom_call" | custom-call | flops 8999999488 | bytes 36000000 | tf_op jit(solution)/shard_map/contract/pallas_call | solution.py:300
  (22 shorter events, 0.2 us)
Async XLA Ops:
  0.0 2.2 %collective-permute-start = (bf16[16,2,8192]{2,1,0:T(2,128)(2,1)}, bf16[16,2,8192]{2,1,0:T(2,128)(2,1)S(1)}, u32[]{:S(2)}, u32[]{:S(2)}) collective-permute-start(bf16[16,2,8192]{2,1,0:T(2,128)(2,1)} %param.7), channel_id=1, source_target_pairs={{0,1},{1,0},{2,3},{3,2},{4,5},{5,4},{6,7},{7,6},{8,9},{9,8},{10,11... | collective-permute-start | bytes 1572872 | tf_op jit(solution)/shard_map/ppermute | solution.py:232
  2.2 1.0 %copy-start = (bf16[16,2,8192]{2,1,0:T(2,128)(2,1)S(1)}, bf16[16,2,8192]{2,1,0:T(2,128)(2,1)}, u32[]{:S(2)}) copy-start(bf16[16,2,8192]{2,1,0:T(2,128)(2,1)} %param.7) | copy-start | bytes 1572868
  3.3 0.9 copy-start.2
  4.2 0.7 copy-start.4
  4.9 0.7 copy-start.6
  8.9 9.5 %collective-permute-start.1 = (bf16[32,32,128]{2,1,0:T(8,128)(2,1)S(1)}, bf16[32,32,128]{2,1,0:T(8,128)(2,1)S(1)}, u32[]{:S(2)}, u32[]{:S(2)}) collective-permute-start(bf16[32,32,128]{2,1,0:T(8,128)(2,1)S(1)} %pad_maximum_fusion), channel_id=1, source_target_pairs={{0,2},{2,0},{4,6},{6,4},{8,10},{10,8},{12,14},{14,12},{1,3},{3,1},... | collective-permute-start | bytes 786440 | tf_op jit(solution)/shard_map/ppermute | solution.py:235
  11.9 21.4 %collective-permute-start.6 = (bf16[16,2,4096]{2,1,0:T(2,128)(2,1)}, bf16[16,2,4096]{2,1,0:T(2,128)(2,1)S(1)}, u32[]{:S(2)}, u32[]{:S(2)}) collective-permute-start(bf16[16,2,4096]{2,1,0:T(2,128)(2,1)} %param.8), channel_id=1, source_target_pairs={{0,1},{1,0},{2,3},{3,2},{4,5},{5,4},{6,7},{7,6},{8,9},{9,8},{10,11... | collective-permute-start | bytes 786440 | tf_op jit(solution)/shard_map/ppermute | solution.py:232
  18.5 6.4 %collective-permute-start.2 = (bf16[16,32,128]{2,1,0:T(8,128)(2,1)S(1)}, bf16[16,32,128]{2,1,0:T(8,128)(2,1)S(1)}, u32[]{:S(2)}, u32[]{:S(2)}) collective-permute-start(bf16[16,32,128]{2,1,0:T(8,128)(2,1)S(1)} %pad_maximum_fusion.1), channel_id=1, source_target_pairs={{0,4},{2,6},{4,0},{6,2},{8,12},{10,14},{12,8},{14,10},{1,5},{3,7},... | collective-permute-start | bytes 393224 | tf_op jit(solution)/shard_map/ppermute | solution.py:235
  20.4 12.4 %collective-permute-start.3 = (bf16[16,32,128]{2,1,0:T(8,128)(2,1)S(1)}, bf16[16,32,128]{2,1,0:T(8,128)(2,1)S(1)}, u32[]{:S(2)}, u32[]{:S(2)}) collective-permute-start(bf16[16,32,128]{2,1,0:T(8,128)(2,1)S(1)} %pad_maximum_fusion.2), channel_id=1, source_target_pairs={{0,8},{2,10},{4,12},{6,14},{8,0},{10,2},{12,4},{14,6},{1,9},{3,11}... | collective-permute-start | bytes 393224 | tf_op jit(solution)/shard_map/ppermute | solution.py:235
  23.1 9.7 %collective-permute-start.4 = (bf16[16,32,128]{2,1,0:T(8,128)(2,1)S(1)}, bf16[16,32,128]{2,1,0:T(8,128)(2,1)S(1)}, u32[]{:S(2)}, u32[]{:S(2)}) collective-permute-start(bf16[16,32,128]{2,1,0:T(8,128)(2,1)S(1)} %pad_maximum_fusion.3), channel_id=1, source_target_pairs={{0,12},{2,14},{4,8},{6,10},{8,4},{10,6},{12,0},{14,2},{1,13},{3,15... | collective-permute-start | bytes 393224 | tf_op jit(solution)/shard_map/ppermute | solution.py:235
  33.2 46.0 %collective-permute-start.5 = (bf16[2,1024,256]{2,1,0:T(8,128)(2,1)S(1)}, bf16[2,1024,256]{2,1,0:T(8,128)(2,1)S(1)}, u32[]{:S(2)}, u32[]{:S(2)}) collective-permute-start(bf16[2,1024,256]{2,1,0:T(8,128)(2,1)S(1)} %left_arrange.1.refs_0_), channel_id=1, source_target_pairs={{0,1},{1,0},{2,3},{3,2},{4,5},{5,4},{6,7},{7,6},{8,9},{9,8},{10,11... | collective-permute-start | bytes 3145736 | tf_op jit(solution)/shard_map/ppermute | solution.py:232
  33.3 1.0 %copy-start.1 = (bf16[16,2,4096]{2,1,0:T(2,128)(2,1)S(1)}, bf16[16,2,4096]{2,1,0:T(2,128)(2,1)}, u32[]{:S(2)}) copy-start(bf16[16,2,4096]{2,1,0:T(2,128)(2,1)} %param.8) | copy-start | bytes 786436
  34.2 0.9 copy-start.3
  35.1 0.7 copy-start.5
  38.6 15.7 %collective-permute-start.10 = (bf16[32,32,128]{2,1,0:T(8,128)(2,1)S(1)}, bf16[32,32,128]{2,1,0:T(8,128)(2,1)S(1)}, u32[]{:S(2)}, u32[]{:S(2)}) collective-permute-start(bf16[32,32,128]{2,1,0:T(8,128)(2,1)S(1)} %right_prep.1.refs_2_), channel_id=1, source_target_pairs={{0,8},{2,10},{4,12},{6,14},{8,0},{10,2},{12,4},{14,6},{1,9},{3,11}... | collective-permute-start | bytes 786440 | tf_op jit(solution)/shard_map/ppermute | solution.py:235
  41.6 14.7 %collective-permute-start.8 = (bf16[32,32,128]{2,1,0:T(8,128)(2,1)S(1)}, bf16[32,32,128]{2,1,0:T(8,128)(2,1)S(1)}, u32[]{:S(2)}, u32[]{:S(2)}) collective-permute-start(bf16[32,32,128]{2,1,0:T(8,128)(2,1)S(1)} %right_prep.1.refs_2_), channel_id=1, source_target_pairs={{0,4},{2,6},{4,0},{6,2},{8,12},{10,14},{12,8},{14,10},{1,5},{3,7},... | collective-permute-start | bytes 786440 | tf_op jit(solution)/shard_map/ppermute | solution.py:235
  54.3 8.1 %collective-permute-start.12 = (bf16[32,32,128]{2,1,0:T(8,128)(2,1)S(1)}, bf16[32,32,128]{2,1,0:T(8,128)(2,1)S(1)}, u32[]{:S(2)}, u32[]{:S(2)}) collective-permute-start(bf16[32,32,128]{2,1,0:T(8,128)(2,1)S(1)} %collective-permute-done.10.refs_6_), channel_id=1, source_target_pairs={{0,4},{2,6},{4,0},{6,2},{8,12},{10,14},{12,8},{14,10},{1,5},{3,7},... | collective-permute-start | bytes 786440 | tf_op jit(solution)/shard_map/ppermute | solution.py:235
  54.3 9.6 %collective-permute-start.7 = (bf16[32,32,128]{2,1,0:T(8,128)(2,1)S(1)}, bf16[32,32,128]{2,1,0:T(8,128)(2,1)S(1)}, u32[]{:S(2)}, u32[]{:S(2)}) collective-permute-start(bf16[32,32,128]{2,1,0:T(8,128)(2,1)S(1)} %right_prep.1.refs_2_), channel_id=1, source_target_pairs={{0,2},{2,0},{4,6},{6,4},{8,10},{10,8},{12,14},{14,12},{1,3},{3,1},... | collective-permute-start | bytes 786440 | tf_op jit(solution)/shard_map/ppermute | solution.py:235
  55.8 13.3 %collective-permute-start.11 = (bf16[32,32,128]{2,1,0:T(8,128)(2,1)S(1)}, bf16[32,32,128]{2,1,0:T(8,128)(2,1)S(1)}, u32[]{:S(2)}, u32[]{:S(2)}) collective-permute-start(bf16[32,32,128]{2,1,0:T(8,128)(2,1)S(1)} %collective-permute-done.10.refs_6_), channel_id=1, source_target_pairs={{0,2},{2,0},{4,6},{6,4},{8,10},{10,8},{12,14},{14,12},{1,3},{3,1},... | collective-permute-start | bytes 786440 | tf_op jit(solution)/shard_map/ppermute | solution.py:235
  56.3 18.4 %collective-permute-start.9 = (bf16[32,32,128]{2,1,0:T(8,128)(2,1)S(1)}, bf16[32,32,128]{2,1,0:T(8,128)(2,1)S(1)}, u32[]{:S(2)}, u32[]{:S(2)}) collective-permute-start(bf16[32,32,128]{2,1,0:T(8,128)(2,1)S(1)} %collective-permute-done.8.refs_4_), channel_id=1, source_target_pairs={{0,2},{2,0},{4,6},{6,4},{8,10},{10,8},{12,14},{14,12},{1,3},{3,1},... | collective-permute-start | bytes 786440 | tf_op jit(solution)/shard_map/ppermute | solution.py:235
  62.4 16.9 %collective-permute-start.13 = (bf16[32,32,128]{2,1,0:T(8,128)(2,1)S(1)}, bf16[32,32,128]{2,1,0:T(8,128)(2,1)S(1)}, u32[]{:S(2)}, u32[]{:S(2)}) collective-permute-start(bf16[32,32,128]{2,1,0:T(8,128)(2,1)S(1)} %collective-permute-done.12.refs_8_), channel_id=1, source_target_pairs={{0,2},{2,0},{4,6},{6,4},{8,10},{10,8},{12,14},{14,12},{1,3},{3,1},... | collective-permute-start | bytes 786440 | tf_op jit(solution)/shard_map/ppermute | solution.py:235
where the time goes:
time: 92.2 us; the launch traced here: 91.9 us
  waiting for transfers between devices  50.4 us (55%)
  Pallas kernels  19.1 us (21%)
  starting transfers between devices  16.3 us (18%)
  local copies, waits for them, and re-layouts  5.87 us (6%)
    ppermute x11, waiting for transfers between devices, hop(): return lax.ppermute(x, 'path', [(i, i ^ k) for i in range(count)])  48.7 us
    ppermute x11, starting transfers between devices, hop(): return lax.ppermute(x, 'path', [(i, i ^ k) for i in range(count)])  15.7 us
    pallas_call x1, Pallas kernels, shards(): pl.pallas_call(lambda *refs: contract_kernel(count, step, *refs), in_spec...  12.7 us
    unnamed x14, local copies, waits for them, and re-layouts  5.82 us
    pallas_call x1, Pallas kernels, shards(): pl.pallas_call(lambda *refs: left_kernel(count, *refs), in_specs=[SMEM, S...  3.35 us
    pallas_call x1, Pallas kernels, shards(): pl.pallas_call(right_kernel, in_specs=[SMEM, SMEM, VMEM, VMEM, VMEM], out...  2.73 us
  transfers between devices with their start and end apart: 14, of which 9 were waited for; matrix products, arithmetic and copies ran while one was open for 0% of the time, Pallas kernels for 3%

commit v1 on v0

--- a/solution.py
+++ b/solution.py
@@ -1,3 +1,5 @@
+import functools
+
 import jax
 import jax.numpy as jnp
 from jax import lax
@@ -49,13 +51,14 @@
     return jnp.concatenate([top, bottom], 0).astype(BF16)
 
 
-def cut_and_low(rows, path, index_ref, terms_ref, gates_ref):
+def cut_and_low(rows, path, table, index_ref, terms_ref, gates_ref):
     width = rows.shape[1]
     term = index_ref[path]
     parity = iota((1, width), 1) % 2 == 0
 
     def pattern(part, first, second):
-        return jnp.where(parity, terms_ref[part, 0, first, term], terms_ref[part, 1, second, term])
+        at = table + 4 * part
+        return jnp.where(parity, terms_ref[at + first, term], terms_ref[at + 2 + second, term])
 
     sign = row_sign(rows.shape)
     value = rows.astype(F32)
@@ -71,9 +74,10 @@
     return (low[:, :width] + swap_rows(low[:, width:]) * sign).astype(BF16)
 
 
-def left_kernel(count, index_ref, terms_ref, gates_ref, own_ref, other_ref, *rest):
+def left_kernel(count, index_ref, terms_ref, gates_ref, slabs_ref, other_ref, *rest):
     out_refs, stage = rest[:count], rest[count]
-    paths, _, width = own_ref.shape
+    paths, size, width = other_ref.shape
+    own_ref = slabs_ref.at[:, :size]
     mine, core = lax.axis_index("path"), lax.axis_index("amp")
     half = width // 2
     part = half // count
@@ -89,7 +93,7 @@
         columns = []
         for path in (pair, pair + 1):
             parts = [
-                cut_and_low(ref[path], path, index_ref, terms_ref, gates_ref)
+                cut_and_low(ref[path], path, 8, index_ref, terms_ref, gates_ref)
                 for ref in (own_ref, other_ref)
             ]
             columns.append(jnp.concatenate(parts, 0))
@@ -104,8 +108,9 @@
         out_refs[k][...] = rows.astype(BF16).reshape(part, slots, width)
 
 
-def right_kernel(index_ref, terms_ref, gates_ref, own_ref, other_ref, out_ref, stage):
-    paths, _, width = own_ref.shape
+def right_kernel(index_ref, terms_ref, gates_ref, slabs_ref, other_ref, out_ref, stage):
+    paths, size, width = other_ref.shape
+    own_ref = slabs_ref.at[:, slabs_ref.shape[1] - size :]
     core = lax.axis_index("amp")
     half, quarter = width // 2, width // 4
     which = iota((half, width), 0)
@@ -124,7 +129,7 @@
             first, second = [
                 jnp.concatenate(
                     [
-                        cut_and_low(ref[path], path, index_ref, terms_ref, gates_ref)
+                        cut_and_low(ref[path], path, 0, index_ref, terms_ref, gates_ref)
                         for ref in (own_ref, other_ref)
                     ],
                     0,
@@ -149,13 +154,13 @@
 
 
 def arrange_kernel(count, *refs):
-    pieces, out_ref = refs[:count], refs[count]
-    part, slots, width = pieces[0].shape
+    blocks, out_ref = refs[:count], refs[count]
+    part, slots, width = blocks[0].shape
     paths = slots // 2
     for j in range(part):
         plain, crossed = [], []
-        for piece in pieces:
-            block = piece[j].astype(F32)
+        for ref in blocks:
+            block = ref[j].astype(F32)
             real, imag = block[:paths], block[paths:]
             plain += [real, -imag]
             crossed += [imag, real]
@@ -214,6 +219,7 @@
 SMEM = pl.BlockSpec(memory_space=pltpu.SMEM)
 VMEM = pl.BlockSpec(memory_space=pltpu.VMEM)
 ANY = pl.BlockSpec(memory_space=pl.ANY)
+HBM = pl.BlockSpec(memory_space=pltpu.HBM)
 
 
 def as_rows(slab, width):
@@ -238,6 +244,11 @@
     left_other = swap(left_slabs)
 
     groups = right_slabs.shape[2] // width
+    part = width // 2 // count
+    slabs = as_rows(jnp.concatenate([left_slabs, right_slabs], 2), width)
+    terms = jnp.concatenate(
+        [terms.transpose(1, 2, 3, 0).reshape(8, -1) for terms in (right_terms, left_terms)], 0
+    )
     right = pl.pallas_call(
         right_kernel,
         in_specs=[SMEM, SMEM, VMEM, VMEM, VMEM],
@@ -247,17 +258,9 @@
         cost_estimate=pl.CostEstimate(flops=2 * 10**9, bytes_accessed=10**6, transcendentals=0),
         compiler_params=pltpu.CompilerParams(vmem_limit_bytes=24 * 2**20),
         name="right_prep",
-    )(
-        term_index,
-        right_terms.transpose(1, 2, 3, 0),
-        right_gates,
-        as_rows(right_slabs, width),
-        as_rows(right_other, width),
-    )
-
-    part = width // 2 // count
+    )(term_index, terms, right_gates, slabs, as_rows(right_other, width))
     left = pl.pallas_call(
-        lambda *refs: left_kernel(count, *refs),
+        functools.partial(left_kernel, count),
         in_specs=[SMEM, SMEM, VMEM, VMEM, VMEM],
         out_specs=[VMEM] * count,
         out_shape=[jax.ShapeDtypeStruct((part, slots, width), BF16)] * count,
@@ -265,7 +268,7 @@
         cost_estimate=pl.CostEstimate(flops=4 * 10**9, bytes_accessed=2 * 10**6, transcendentals=0),
         compiler_params=pltpu.CompilerParams(vmem_limit_bytes=24 * 2**20),
         name="left_prep",
-    )(term_index, left_terms.transpose(1, 2, 3, 0), left_gates, as_rows(left_slabs, width), as_rows(left_other, width))
+    )(term_index, terms, left_gates, slabs, as_rows(left_other, width))
 
     pieces = {0: right}
     bit = count // 2
@@ -283,19 +286,17 @@
         if k:
             both = hop(both, k)
         blocks[k], blocks[k + 1] = both[:part], both[part:]
-    blocks = [blocks[k] for k in range(count)]
     rows = part * width
     own = pl.pallas_call(
-        lambda *refs: arrange_kernel(count, *refs),
+        functools.partial(arrange_kernel, count),
         in_specs=[VMEM] * count,
         out_specs=VMEM,
         out_shape=jax.ShapeDtypeStruct((2, rows, count * slots), BF16),
-        cost_estimate=pl.CostEstimate(flops=2 * 10**9, bytes_accessed=10**6, transcendentals=0),
+        cost_estimate=pl.CostEstimate(flops=10**9, bytes_accessed=10**6, transcendentals=0),
         compiler_params=pltpu.CompilerParams(vmem_limit_bytes=16 * 2**20),
         name="left_arrange",
-    )(*blocks)
+    )(*[blocks[k] for k in range(count)])
     other = swap(own)
-
     step = 4
     return pl.pallas_call(
         lambda *refs: contract_kernel(count, step, *refs),

time: 92.2 us -> 86.6 us (0.939)
  local copies, waits for them, and re-layouts: 5.87 us -> 0.53 us
  waiting for transfers between devices: 50.4 us -> 48.3 us
  other arithmetic: 0.08 us -> 2.08 us
    unnamed x14 -> x12, local copies, waits for them, and re-layouts: 5.82 us -> 0.49 us
    concatenate x0 -> x2, other arithmetic: none -> 2 us  [the longest x1 2 us: shards(): slabs = as_rows(jnp.concatenate([left_slabs, right_slabs], 2), width)]
    ppermute x3, waiting for transfers between devices: 1.75 us -> 0.01 us  [swap(): return lax.ppermute(x, 'amp', [(0, 1), (1, 0)])]
  transfers between devices with their start and end apart: 14 -> 14, of which waited for: 9 -> 9; matrix products, arithmetic and copies ran while one was open for 0% -> 2% of each run, Pallas kernels for 3% -> 4%
where the time goes in v1:
time: 86.6 us; the launch traced here: 86.5 us
  waiting for transfers between devices  48.3 us (56%)
  Pallas kernels  19.2 us (22%)
  starting transfers between devices  16.1 us (19%)
  other arithmetic  2.08 us (2%)
    ppermute x11, waiting for transfers between devices, hop(): return lax.ppermute(x, 'path', [(i, i ^ k) for i in range(count)])  48.3 us
    ppermute x11, starting transfers between devices, hop(): return lax.ppermute(x, 'path', [(i, i ^ k) for i in range(count)])  15.3 us
    pallas_call x1, Pallas kernels, shards(): pl.pallas_call(lambda *refs: contract_kernel(count, step, *refs), in_spec...  12.7 us
    pallas_call x1, Pallas kernels, shards(): pl.pallas_call(functools.partial(left_kernel, count), in_specs=[SMEM, SME...  3.43 us
    pallas_call x1, Pallas kernels, shards(): pl.pallas_call(right_kernel, in_specs=[SMEM, SMEM, VMEM, VMEM, VMEM], out...  2.8 us
    concatenate x1, other arithmetic, shards(): slabs = as_rows(jnp.concatenate([left_slabs, right_slabs], 2), width)  2 us
  transfers between devices with their start and end apart: 14, of which 9 were waited for; matrix products, arithmetic and copies ran while one was open for 2% of the time, Pallas kernels for 4%

profile of v1, /device:TPU:0, one launch (start us, length us, event | category | flops | bytes accessed | tf_op | source)
XLA Modules:
  0.0 86.5 jit_solution(8308837148725095334)
XLA Ops:
  0.0 0.6 collective-permute-start
  0.6 2.0 %pad_maximum_fusion = bf16[16,2,12288]{2,1,0:T(2,128)(2,1)S(1)} fusion(bf16[16,2,4096]{2,1,0:T(2,128)(2,1)} %param.8, bf16[16,2,8192]{2,1,0:T(2,128)(2,1)} %param.7), kind=kLoop, calls=%fused_computation | loop fusion | flops 1572864 | bytes 1572864 | tf_op jit(solution)/shard_map/concatenate | solution.py:248
  2.6 0.0 collective-permute-done
  2.6 0.0 copy-start.3
  2.7 3.4 %left_prep.1 = (bf16[8,32,128]{2,1,0:T(8,128)(2,1)S(1)}, bf16[8,32,128]{2,1,0:T(8,128)(2,1)S(1)}, bf16[8,32,128]{2,1,0:T(8,128)(2,1)S(1)}, bf16[8,32,128]{2,1,0:...) custom-call(s32[16]{0:T(128)S(1)} %copy-done.2, ...), custom_call_target="tpu_custom_call" | custom-call | flops 4000000000 | bytes 2000000 | tf_op jit(solution)/shard_map/left_prep/pallas_call | solution.py:262
  6.1 2.6 %collective-permute-start.1 = (bf16[32,32,128]{2,1,0:T(8,128)(2,1)S(1)}, bf16[32,32,128]{2,1,0:T(8,128)(2,1)S(1)}, u32[]{:S(2)}, u32[]{:S(2)}) collective-permute-start(bf16[32,32,128]{2,1,0:T(8,128)(2,1)S(1)} %pad_maximum_fusion.1), channel_id=1, source_target_pairs={{0,2},{2,0},{4,6},{6,4},{8,10},{10,8},{12,14},{14,12},{1,3},{3,1},... | collective-permute-start | bytes 786440 | tf_op jit(solution)/shard_map/ppermute | solution.py:241
  8.8 0.2 collective-permute-start.6
  8.9 6.7 %collective-permute-done.1 = bf16[32,32,128]{2,1,0:T(8,128)(2,1)S(1)} collective-permute-done((bf16[32,32,128]{2,1,0:T(8,128)(2,1)S(1)}, bf16[32,32,128]{2,1,0:T(8,128)(2,1)S(1)}, u32[]{:S(2)}, u32[]{:S(2)}) %collective-permute-start.1) | collective-permute-done | bytes 262176 | tf_op jit(solution)/shard_map/ppermute | solution.py:241
  15.7 1.9 %collective-permute-start.2 = (bf16[16,32,128]{2,1,0:T(8,128)(2,1)S(1)}, bf16[16,32,128]{2,1,0:T(8,128)(2,1)S(1)}, u32[]{:S(2)}, u32[]{:S(2)}) collective-permute-start(bf16[16,32,128]{2,1,0:T(8,128)(2,1)S(1)} %pad_maximum_fusion.2), channel_id=1, source_target_pairs={{0,4},{2,6},{4,0},{6,2},{8,12},{10,14},{12,8},{14,10},{1,5},{3,7},... | collective-permute-start | bytes 393224 | tf_op jit(solution)/shard_map/ppermute | solution.py:241
  17.6 2.7 %collective-permute-start.3 = (bf16[16,32,128]{2,1,0:T(8,128)(2,1)S(1)}, bf16[16,32,128]{2,1,0:T(8,128)(2,1)S(1)}, u32[]{:S(2)}, u32[]{:S(2)}) collective-permute-start(bf16[16,32,128]{2,1,0:T(8,128)(2,1)S(1)} %pad_maximum_fusion.3), channel_id=1, source_target_pairs={{0,8},{2,10},{4,12},{6,14},{8,0},{10,2},{12,4},{14,6},{1,9},{3,11}... | collective-permute-start | bytes 393224 | tf_op jit(solution)/shard_map/ppermute | solution.py:241
  20.3 0.1 collective-permute-start.4
  20.4 2.2 %collective-permute-done.2 = bf16[16,32,128]{2,1,0:T(8,128)(2,1)S(1)} collective-permute-done((bf16[16,32,128]{2,1,0:T(8,128)(2,1)S(1)}, bf16[16,32,128]{2,1,0:T(8,128)(2,1)S(1)}, u32[]{:S(2)}, u32[]{:S(2)}) %collective-permute-start.2) | collective-permute-done | bytes 131104 | tf_op jit(solution)/shard_map/ppermute | solution.py:241
  22.6 7.7 %collective-permute-done.3 = bf16[16,32,128]{2,1,0:T(8,128)(2,1)S(1)} collective-permute-done((bf16[16,32,128]{2,1,0:T(8,128)(2,1)S(1)}, bf16[16,32,128]{2,1,0:T(8,128)(2,1)S(1)}, u32[]{:S(2)}, u32[]{:S(2)}) %collective-permute-start.3) | collective-permute-done | bytes 131104 | tf_op jit(solution)/shard_map/ppermute | solution.py:241
  30.4 0.0 copy-start.1
  30.4 0.3 left_arrange.1.refs_0_
  30.7 0.1 collective-permute-start.5
  30.8 0.5 copy-done.1
  31.3 2.8 %right_prep.1.refs_2_ = bf16[32,32,128]{2,1,0:T(8,128)(2,1)S(1)} custom-call(s32[16]{0:T(128)S(1)} %copy-done.2, f32[16,4]{1,0:T(8,128)S(1)} %pad_maximum_fusion.5.terms_ref, bf16[2,2,128,128]{3,2,1,0:T(8,128)(2,1)S(1)} %copy-done.1, bf16[16,192,128]{2,1,0:T(8,128)(2,1)S(1)} %bitcast.22, bf16[16,64,128]{2,1,0:T(8,128)(2,1)S(1)} %bitcast.24), custom_call_target="tpu_custom_call" | custom-call | flops 2000000000 | bytes 1000000 | tf_op jit(solution)/shard_map/right_prep/pallas_call | solution.py:252
  34.1 3.1 %collective-permute-start.10 = (bf16[32,32,128]{2,1,0:T(8,128)(2,1)S(1)}, bf16[32,32,128]{2,1,0:T(8,128)(2,1)S(1)}, u32[]{:S(2)}, u32[]{:S(2)}) collective-permute-start(bf16[32,32,128]{2,1,0:T(8,128)(2,1)S(1)} %right_prep.1.refs_2_), channel_id=1, source_target_pairs={{0,8},{2,10},{4,12},{6,14},{8,0},{10,2},{12,4},{14,6},{1,9},{3,11}... | collective-permute-start | bytes 786440 | tf_op jit(solution)/shard_map/ppermute | solution.py:241
  37.1 0.0 collective-permute-start.8
  37.2 12.2 %collective-permute-done.10.refs_6_ = bf16[32,32,128]{2,1,0:T(8,128)(2,1)S(1)} collective-permute-done((bf16[32,32,128]{2,1,0:T(8,128)(2,1)S(1)}, bf16[32,32,128]{2,1,0:T(8,128)(2,1)S(1)}, u32[]{:S(2)}, u32[]{:S(2)}) %collective-permute-start.10) | collective-permute-done | bytes 262176 | tf_op jit(solution)/shard_map/ppermute | solution.py:241
  49.4 1.5 %collective-permute-start.7 = (bf16[32,32,128]{2,1,0:T(8,128)(2,1)S(1)}, bf16[32,32,128]{2,1,0:T(8,128)(2,1)S(1)}, u32[]{:S(2)}, u32[]{:S(2)}) collective-permute-start(bf16[32,32,128]{2,1,0:T(8,128)(2,1)S(1)} %right_prep.1.refs_2_), channel_id=1, source_target_pairs={{0,2},{2,0},{4,6},{6,4},{8,10},{10,8},{12,14},{14,12},{1,3},{3,1},... | collective-permute-start | bytes 786440 | tf_op jit(solution)/shard_map/ppermute | solution.py:241
  50.9 0.5 collective-permute-start.11
  51.4 0.0 collective-permute-done.8.refs_4_
  51.4 1.5 %collective-permute-start.9 = (bf16[32,32,128]{2,1,0:T(8,128)(2,1)S(1)}, bf16[32,32,128]{2,1,0:T(8,128)(2,1)S(1)}, u32[]{:S(2)}, u32[]{:S(2)}) collective-permute-start(bf16[32,32,128]{2,1,0:T(8,128)(2,1)S(1)} %collective-permute-done.8.refs_4_), channel_id=1, source_target_pairs={{0,2},{2,0},{4,6},{6,4},{8,10},{10,8},{12,14},{14,12},{1,3},{3,1},... | collective-permute-start | bytes 786440 | tf_op jit(solution)/shard_map/ppermute | solution.py:241
  52.9 4.1 %collective-permute-done.12.refs_8_ = bf16[32,32,128]{2,1,0:T(8,128)(2,1)S(1)} collective-permute-done((bf16[32,32,128]{2,1,0:T(8,128)(2,1)S(1)}, bf16[32,32,128]{2,1,0:T(8,128)(2,1)S(1)}, u32[]{:S(2)}, u32[]{:S(2)}) %collective-permute-start.12) | collective-permute-done | bytes 262176 | tf_op jit(solution)/shard_map/ppermute | solution.py:241
  57.0 1.5 %collective-permute-start.13 = (bf16[32,32,128]{2,1,0:T(8,128)(2,1)S(1)}, bf16[32,32,128]{2,1,0:T(8,128)(2,1)S(1)}, u32[]{:S(2)}, u32[]{:S(2)}) collective-permute-start(bf16[32,32,128]{2,1,0:T(8,128)(2,1)S(1)} %collective-permute-done.12.refs_8_), channel_id=1, source_target_pairs={{0,2},{2,0},{4,6},{6,4},{8,10},{10,8},{12,14},{14,12},{1,3},{3,1},... | collective-permute-start | bytes 786440 | tf_op jit(solution)/shard_map/ppermute | solution.py:241
  58.5 0.1 collective-permute-done.7.refs_3_
  58.5 5.6 %collective-permute-done.11.refs_7_ = bf16[32,32,128]{2,1,0:T(8,128)(2,1)S(1)} collective-permute-done((bf16[32,32,128]{2,1,0:T(8,128)(2,1)S(1)}, bf16[32,32,128]{2,1,0:T(8,128)(2,1)S(1)}, u32[]{:S(2)}, u32[]{:S(2)}) %collective-permute-start.11) | collective-permute-done | bytes 262176 | tf_op jit(solution)/shard_map/ppermute | solution.py:241
  64.2 5.6 %collective-permute-done.9.refs_5_ = bf16[32,32,128]{2,1,0:T(8,128)(2,1)S(1)} collective-permute-done((bf16[32,32,128]{2,1,0:T(8,128)(2,1)S(1)}, bf16[32,32,128]{2,1,0:T(8,128)(2,1)S(1)}, u32[]{:S(2)}, u32[]{:S(2)}) %collective-permute-start.9) | collective-permute-done | bytes 262176 | tf_op jit(solution)/shard_map/ppermute | solution.py:241
  69.8 4.0 %collective-permute-done.13.refs_9_ = bf16[32,32,128]{2,1,0:T(8,128)(2,1)S(1)} collective-permute-done((bf16[32,32,128]{2,1,0:T(8,128)(2,1)S(1)}, bf16[32,32,128]{2,1,0:T(8,128)(2,1)S(1)}, u32[]{:S(2)}, u32[]{:S(2)}) %collective-permute-start.13) | collective-permute-done | bytes 262176 | tf_op jit(solution)/shard_map/ppermute | solution.py:241
  73.8 12.7 %contract.1 = bf16[2,2048,4096]{2,1,0:T(8,128)(2,1)} custom-call(bf16[2,1024,256]{2,1,0:T(8,128)(2,1)S(1)} %left_arrange.1.refs_0_, bf16[2,1024,256]{2,1,0:T(8,128)(2,1)S(1)} %collective-permute-done.5.refs_1_, bf16[32,32,128]{2,1,0:T(8,128)(2,1)S(1)} %right_prep.1.refs_2_, bf16[32,32,128]{2,1,0:T(8,128)(2,1)S(1)} %collective-permute-done.7.refs_3_, ...), custom_call_target="tpu_custom_call" | custom-call | flops 8999999488 | bytes 36000000 | tf_op jit(solution)/shard_map/contract/pallas_call | solution.py:301
  (22 shorter events, 0.2 us)
Async XLA Ops:
  0.0 2.6 %copy-start.5 = (f32[4,2,2,2]{0,3,2,1:T(2,128)S(1)}, f32[4,2,2,2]{0,3,2,1:T(2,128)}, u32[]{:S(2)}) copy-start(f32[4,2,2,2]{0,3,2,1:T(2,128)} %param.11) | copy-start | bytes 388
  0.0 2.6 %copy-start.4 = (f32[4,2,2,2]{0,3,2,1:T(2,128)S(1)}, f32[4,2,2,2]{0,3,2,1:T(2,128)}, u32[]{:S(2)}) copy-start(f32[4,2,2,2]{0,3,2,1:T(2,128)} %param.10) | copy-start | bytes 388
  0.0 2.6 %copy-start.2 = (s32[16]{0:T(128)S(1)}, s32[16]{0:T(128)}, u32[]{:S(2)}) copy-start(s32[16]{0:T(128)} %index_ref.3) | copy-start | bytes 196
  0.0 2.6 %copy-start = (bf16[2,2,128,128]{3,2,1,0:T(8,128)(2,1)S(1)}, bf16[2,2,128,128]{3,2,1,0:T(8,128)(2,1)}, u32[]{:S(2)}) copy-start(bf16[2,2,128,128]{3,2,1,0:T(8,128)(2,1)} %gates_ref.2) | copy-start | bytes 393220
  0.0 2.6 %collective-permute-start = (bf16[16,2,8192]{2,1,0:T(2,128)(2,1)}, bf16[16,2,8192]{2,1,0:T(2,128)(2,1)S(1)}, u32[]{:S(2)}, u32[]{:S(2)}) collective-permute-start(bf16[16,2,8192]{2,1,0:T(2,128)(2,1)} %param.7), channel_id=1, source_target_pairs={{0,1},{1,0},{2,3},{3,2},{4,5},{5,4},{6,7},{7,6},{8,9},{9,8},{10,11... | collective-permute-start | bytes 1572872 | tf_op jit(solution)/shard_map/ppermute | solution.py:238
  2.6 6.1 %copy-start.3 = (bf16[16,2,4096]{2,1,0:T(2,128)(2,1)S(1)}, bf16[16,2,4096]{2,1,0:T(2,128)(2,1)}, u32[]{:S(2)}) copy-start(bf16[16,2,4096]{2,1,0:T(2,128)(2,1)} %param.8) | copy-start | bytes 786436
  6.1 9.5 %collective-permute-start.1 = (bf16[32,32,128]{2,1,0:T(8,128)(2,1)S(1)}, bf16[32,32,128]{2,1,0:T(8,128)(2,1)S(1)}, u32[]{:S(2)}, u32[]{:S(2)}) collective-permute-start(bf16[32,32,128]{2,1,0:T(8,128)(2,1)S(1)} %pad_maximum_fusion.1), channel_id=1, source_target_pairs={{0,2},{2,0},{4,6},{6,4},{8,10},{10,8},{12,14},{14,12},{1,3},{3,1},... | collective-permute-start | bytes 786440 | tf_op jit(solution)/shard_map/ppermute | solution.py:241
  8.8 22.1 %collective-permute-start.6 = (bf16[16,2,4096]{2,1,0:T(2,128)(2,1)S(1)}, bf16[16,2,4096]{2,1,0:T(2,128)(2,1)S(1)}, u32[]{:S(2)}, u32[]{:S(2)}) collective-permute-start(bf16[16,2,4096]{2,1,0:T(2,128)(2,1)S(1)} %copy-done.3), channel_id=1, source_target_pairs={{0,1},{1,0},{2,3},{3,2},{4,5},{5,4},{6,7},{7,6},{8,9},{9,8},{10,11... | collective-permute-start | bytes 786440 | tf_op jit(solution)/shard_map/ppermute | solution.py:238
  15.7 6.9 %collective-permute-start.2 = (bf16[16,32,128]{2,1,0:T(8,128)(2,1)S(1)}, bf16[16,32,128]{2,1,0:T(8,128)(2,1)S(1)}, u32[]{:S(2)}, u32[]{:S(2)}) collective-permute-start(bf16[16,32,128]{2,1,0:T(8,128)(2,1)S(1)} %pad_maximum_fusion.2), channel_id=1, source_target_pairs={{0,4},{2,6},{4,0},{6,2},{8,12},{10,14},{12,8},{14,10},{1,5},{3,7},... | collective-permute-start | bytes 393224 | tf_op jit(solution)/shard_map/ppermute | solution.py:241
  17.6 12.7 %collective-permute-start.3 = (bf16[16,32,128]{2,1,0:T(8,128)(2,1)S(1)}, bf16[16,32,128]{2,1,0:T(8,128)(2,1)S(1)}, u32[]{:S(2)}, u32[]{:S(2)}) collective-permute-start(bf16[16,32,128]{2,1,0:T(8,128)(2,1)S(1)} %pad_maximum_fusion.3), channel_id=1, source_target_pairs={{0,8},{2,10},{4,12},{6,14},{8,0},{10,2},{12,4},{14,6},{1,9},{3,11}... | collective-permute-start | bytes 393224 | tf_op jit(solution)/shard_map/ppermute | solution.py:241
  20.3 10.1 %collective-permute-start.4 = (bf16[16,32,128]{2,1,0:T(8,128)(2,1)S(1)}, bf16[16,32,128]{2,1,0:T(8,128)(2,1)S(1)}, u32[]{:S(2)}, u32[]{:S(2)}) collective-permute-start(bf16[16,32,128]{2,1,0:T(8,128)(2,1)S(1)} %pad_maximum_fusion.4), channel_id=1, source_target_pairs={{0,12},{2,14},{4,8},{6,10},{8,4},{10,6},{12,0},{14,2},{1,13},{3,15... | collective-permute-start | bytes 393224 | tf_op jit(solution)/shard_map/ppermute | solution.py:241
  30.4 0.9 %copy-start.1 = (bf16[2,2,128,128]{3,2,1,0:T(8,128)(2,1)S(1)}, bf16[2,2,128,128]{3,2,1,0:T(8,128)(2,1)}, u32[]{:S(2)}) copy-start(bf16[2,2,128,128]{3,2,1,0:T(8,128)(2,1)} %gates_ref.3) | copy-start | bytes 393220
  30.7 43.1 %collective-permute-start.5 = (bf16[2,1024,256]{2,1,0:T(8,128)(2,1)S(1)}, bf16[2,1024,256]{2,1,0:T(8,128)(2,1)S(1)}, u32[]{:S(2)}, u32[]{:S(2)}) collective-permute-start(bf16[2,1024,256]{2,1,0:T(8,128)(2,1)S(1)} %left_arrange.1.refs_0_), channel_id=1, source_target_pairs={{0,1},{1,0},{2,3},{3,2},{4,5},{5,4},{6,7},{7,6},{8,9},{9,8},{10,11... | collective-permute-start | bytes 3145736 | tf_op jit(solution)/shard_map/ppermute | solution.py:238
  34.1 15.3 %collective-permute-start.10 = (bf16[32,32,128]{2,1,0:T(8,128)(2,1)S(1)}, bf16[32,32,128]{2,1,0:T(8,128)(2,1)S(1)}, u32[]{:S(2)}, u32[]{:S(2)}) collective-permute-start(bf16[32,32,128]{2,1,0:T(8,128)(2,1)S(1)} %right_prep.1.refs_2_), channel_id=1, source_target_pairs={{0,8},{2,10},{4,12},{6,14},{8,0},{10,2},{12,4},{14,6},{1,9},{3,11}... | collective-permute-start | bytes 786440 | tf_op jit(solution)/shard_map/ppermute | solution.py:241
  37.1 14.3 %collective-permute-start.8 = (bf16[32,32,128]{2,1,0:T(8,128)(2,1)S(1)}, bf16[32,32,128]{2,1,0:T(8,128)(2,1)S(1)}, u32[]{:S(2)}, u32[]{:S(2)}) collective-permute-start(bf16[32,32,128]{2,1,0:T(8,128)(2,1)S(1)} %right_prep.1.refs_2_), channel_id=1, source_target_pairs={{0,4},{2,6},{4,0},{6,2},{8,12},{10,14},{12,8},{14,10},{1,5},{3,7},... | collective-permute-start | bytes 786440 | tf_op jit(solution)/shard_map/ppermute | solution.py:241
  49.4 7.6 %collective-permute-start.12 = (bf16[32,32,128]{2,1,0:T(8,128)(2,1)S(1)}, bf16[32,32,128]{2,1,0:T(8,128)(2,1)S(1)}, u32[]{:S(2)}, u32[]{:S(2)}) collective-permute-start(bf16[32,32,128]{2,1,0:T(8,128)(2,1)S(1)} %collective-permute-done.10.refs_6_), channel_id=1, source_target_pairs={{0,4},{2,6},{4,0},{6,2},{8,12},{10,14},{12,8},{14,10},{1,5},{3,7},... | collective-permute-start | bytes 786440 | tf_op jit(solution)/shard_map/ppermute | solution.py:241
  49.4 9.2 %collective-permute-start.7 = (bf16[32,32,128]{2,1,0:T(8,128)(2,1)S(1)}, bf16[32,32,128]{2,1,0:T(8,128)(2,1)S(1)}, u32[]{:S(2)}, u32[]{:S(2)}) collective-permute-start(bf16[32,32,128]{2,1,0:T(8,128)(2,1)S(1)} %right_prep.1.refs_2_), channel_id=1, source_target_pairs={{0,2},{2,0},{4,6},{6,4},{8,10},{10,8},{12,14},{14,12},{1,3},{3,1},... | collective-permute-start | bytes 786440 | tf_op jit(solution)/shard_map/ppermute | solution.py:241
  50.9 13.3 %collective-permute-start.11 = (bf16[32,32,128]{2,1,0:T(8,128)(2,1)S(1)}, bf16[32,32,128]{2,1,0:T(8,128)(2,1)S(1)}, u32[]{:S(2)}, u32[]{:S(2)}) collective-permute-start(bf16[32,32,128]{2,1,0:T(8,128)(2,1)S(1)} %collective-permute-done.10.refs_6_), channel_id=1, source_target_pairs={{0,2},{2,0},{4,6},{6,4},{8,10},{10,8},{12,14},{14,12},{1,3},{3,1},... | collective-permute-start | bytes 786440 | tf_op jit(solution)/shard_map/ppermute | solution.py:241
  51.4 18.4 %collective-permute-start.9 = (bf16[32,32,128]{2,1,0:T(8,128)(2,1)S(1)}, bf16[32,32,128]{2,1,0:T(8,128)(2,1)S(1)}, u32[]{:S(2)}, u32[]{:S(2)}) collective-permute-start(bf16[32,32,128]{2,1,0:T(8,128)(2,1)S(1)} %collective-permute-done.8.refs_4_), channel_id=1, source_target_pairs={{0,2},{2,0},{4,6},{6,4},{8,10},{10,8},{12,14},{14,12},{1,3},{3,1},... | collective-permute-start | bytes 786440 | tf_op jit(solution)/shard_map/ppermute | solution.py:241
  57.0 16.9 %collective-permute-start.13 = (bf16[32,32,128]{2,1,0:T(8,128)(2,1)S(1)}, bf16[32,32,128]{2,1,0:T(8,128)(2,1)S(1)}, u32[]{:S(2)}, u32[]{:S(2)}) collective-permute-start(bf16[32,32,128]{2,1,0:T(8,128)(2,1)S(1)} %collective-permute-done.12.refs_8_), channel_id=1, source_target_pairs={{0,2},{2,0},{4,6},{6,4},{8,10},{10,8},{12,14},{14,12},{1,3},{3,1},... | collective-permute-start | bytes 786440 | tf_op jit(solution)/shard_map/ppermute | solution.py:241

commit v2 on v1

--- a/solution.py
+++ b/solution.py
@@ -169,32 +169,23 @@
 
 
 def contract_kernel(count, step, own_ref, other_ref, *refs):
-    pieces, out_ref = refs[:count], refs[count]
-    left, right, staged, in_sems, out_sems = refs[count + 1 :]
+    pieces = refs[:count]
+    out_ref, staged, sems = refs[count:]
     core = lax.axis_index("amp")
     rows = own_ref.shape[1]
-    groups, slots, width = pieces[0].shape
+    groups, _, width = pieces[0].shape
     span = step * width
-    copies = [
-        pltpu.make_async_copy(
-            ref, left.at[:, pl.ds(pl.multiple_of(where * rows, rows), rows), :], in_sems.at[at]
+    tile = min(256, rows)
+    buffers = staged.shape[0]
+
+    def write(i, slot, half, part):
+        place = pl.ds(pl.multiple_of(i * span, span), span)
+        where = pl.ds(pl.multiple_of((core ^ half) * rows, rows), rows)
+        return pltpu.make_async_copy(
+            staged.at[slot, half, part], out_ref.at[part, where, place], sems.at[slot, half, part]
         )
-        for at, (ref, where) in enumerate(((own_ref, core), (other_ref, 1 - core)))
-    ] + [
-        pltpu.make_async_copy(piece, right.at[:, pl.ds(k * slots, slots), :], in_sems.at[2 + k])
-        for k, piece in enumerate(pieces)
-    ]
-    for copy in copies:
-        copy.start()
-    for copy in copies:
-        copy.wait()
-    buffers = staged.shape[0]
-
-    def write(i, slot):
-        place = pl.ds(pl.multiple_of(i * span, span), span)
-        return pltpu.make_async_copy(staged.at[slot], out_ref.at[:, :, place], out_sems.at[slot])
-
-    tile = min(256, 2 * rows)
+
+    quarters = [(half, part) for half in range(2) for part in range(2)]
 
     @pl.loop(0, groups // step)
     def _(i):
@@ -202,18 +193,23 @@
 
         @pl.when(i >= buffers)
         def _():
-            write(i - buffers, slot).wait()
-
-        block = jnp.concatenate([right[i * step + g] for g in range(step)], 1)
-        for part in range(2):
-            for start in range(0, 2 * rows, tile):
-                staged[slot, part, start : start + tile, :] = dot(
-                    left[part, start : start + tile, :], block
+            for quarter in quarters:
+                write(i - buffers, slot, *quarter).wait()
+
+        block = jnp.concatenate(
+            [jnp.concatenate([piece[i * step + g] for piece in pieces], 0) for g in range(step)], 1
+        )
+        for half, part in quarters:
+            ref = (own_ref, other_ref)[half]
+            for start in range(0, rows, tile):
+                staged[slot, half, part, start : start + tile, :] = dot(
+                    ref[part, start : start + tile, :], block
                 ).astype(BF16)
-        write(i, slot).start()
+            write(i, slot, half, part).start()
 
     for i in range(groups // step - buffers, groups // step):
-        write(i, i % buffers).wait()
+        for quarter in quarters:
+            write(i, i % buffers, *quarter).wait()
 
 
 SMEM = pl.BlockSpec(memory_space=pltpu.SMEM)
@@ -300,15 +296,12 @@
     step = 4
     return pl.pallas_call(
         lambda *refs: contract_kernel(count, step, *refs),
-        in_specs=[ANY] * (2 + count),
+        in_specs=[VMEM] * (2 + count),
         out_specs=ANY,
         out_shape=jax.ShapeDtypeStruct((2, 2 * rows, groups * width), BF16),
         scratch_shapes=[
-            pltpu.VMEM((2, 2 * rows, count * slots), BF16),
-            pltpu.VMEM((groups, count * slots, width), BF16),
-            pltpu.VMEM((4, 2, 2 * rows, step * width), BF16),
-            pltpu.SemaphoreType.DMA((2 + count,)),
-            pltpu.SemaphoreType.DMA((4,)),
+            pltpu.VMEM((4, 2, 2, rows, step * width), BF16),
+            pltpu.SemaphoreType.DMA((4, 2, 2)),
         ],
         cost_estimate=pl.CostEstimate(flops=9 * 10**9, bytes_accessed=36 * 10**6, transcendentals=0),
         compiler_params=pltpu.CompilerParams(vmem_limit_bytes=40 * 2**20),

time: 86.6 us -> 85.4 us (0.986)
  Pallas kernels: 19.2 us -> 18 us
    pallas_call x1, Pallas kernels: 12.7 us -> 11.4 us  [shards(): pl.pallas_call(lambda *refs: contract_kernel(count, step, *refs), in_spec...]
where the time goes in v2:
time: 85.4 us; the launch traced here: 85.3 us
  waiting for transfers between devices  48.3 us (57%)
  Pallas kernels  18 us (21%)
  starting transfers between devices  16.1 us (19%)
  other arithmetic  2.08 us (2%)
    ppermute x11, waiting for transfers between devices, hop(): return lax.ppermute(x, 'path', [(i, i ^ k) for i in range(count)])  48.3 us
    ppermute x11, starting transfers between devices, hop(): return lax.ppermute(x, 'path', [(i, i ^ k) for i in range(count)])  15.3 us
    pallas_call x1, Pallas kernels, shards(): pl.pallas_call(lambda *refs: contract_kernel(count, step, *refs), in_spec...  11.4 us
    pallas_call x1, Pallas kernels, shards(): pl.pallas_call(functools.partial(left_kernel, count), in_specs=[SMEM, SME...  3.43 us
    pallas_call x1, Pallas kernels, shards(): pl.pallas_call(right_kernel, in_specs=[SMEM, SMEM, VMEM, VMEM, VMEM], out...  2.8 us
    concatenate x1, other arithmetic, shards(): slabs = as_rows(jnp.concatenate([left_slabs, right_slabs], 2), width)  2 us
  transfers between devices with their start and end apart: 14, of which 9 were waited for; matrix products, arithmetic and copies ran while one was open for 2% of the time, Pallas kernels for 4%

profile of v2, /device:TPU:0, one launch (start us, length us, event | category | flops | bytes accessed | tf_op | source)
XLA Modules:
  0.0 85.3 jit_solution(11782926190000923754)
XLA Ops:
  0.0 0.6 collective-permute-start
  0.6 2.0 %pad_maximum_fusion = bf16[16,2,12288]{2,1,0:T(2,128)(2,1)S(1)} fusion(bf16[16,2,4096]{2,1,0:T(2,128)(2,1)} %param.8, bf16[16,2,8192]{2,1,0:T(2,128)(2,1)} %param.7), kind=kLoop, calls=%fused_computation | loop fusion | flops 1572864 | bytes 1572864 | tf_op jit(solution)/shard_map/concatenate | solution.py:244
  2.6 0.0 collective-permute-done
  2.6 0.0 copy-start.3
  2.7 3.4 %left_prep.1 = (bf16[8,32,128]{2,1,0:T(8,128)(2,1)S(1)}, bf16[8,32,128]{2,1,0:T(8,128)(2,1)S(1)}, bf16[8,32,128]{2,1,0:T(8,128)(2,1)S(1)}, bf16[8,32,128]{2,1,0:...) custom-call(s32[16]{0:T(128)S(1)} %copy-done.2, ...), custom_call_target="tpu_custom_call" | custom-call | flops 4000000000 | bytes 2000000 | tf_op jit(solution)/shard_map/left_prep/pallas_call | solution.py:258
  6.1 2.6 %collective-permute-start.1 = (bf16[32,32,128]{2,1,0:T(8,128)(2,1)S(1)}, bf16[32,32,128]{2,1,0:T(8,128)(2,1)S(1)}, u32[]{:S(2)}, u32[]{:S(2)}) collective-permute-start(bf16[32,32,128]{2,1,0:T(8,128)(2,1)S(1)} %pad_maximum_fusion.1), channel_id=1, source_target_pairs={{0,2},{2,0},{4,6},{6,4},{8,10},{10,8},{12,14},{14,12},{1,3},{3,1},... | collective-permute-start | bytes 786440 | tf_op jit(solution)/shard_map/ppermute | solution.py:237
  8.8 0.2 collective-permute-start.6
  8.9 6.7 %collective-permute-done.1 = bf16[32,32,128]{2,1,0:T(8,128)(2,1)S(1)} collective-permute-done((bf16[32,32,128]{2,1,0:T(8,128)(2,1)S(1)}, bf16[32,32,128]{2,1,0:T(8,128)(2,1)S(1)}, u32[]{:S(2)}, u32[]{:S(2)}) %collective-permute-start.1) | collective-permute-done | bytes 262176 | tf_op jit(solution)/shard_map/ppermute | solution.py:237
  15.7 1.9 %collective-permute-start.2 = (bf16[16,32,128]{2,1,0:T(8,128)(2,1)S(1)}, bf16[16,32,128]{2,1,0:T(8,128)(2,1)S(1)}, u32[]{:S(2)}, u32[]{:S(2)}) collective-permute-start(bf16[16,32,128]{2,1,0:T(8,128)(2,1)S(1)} %pad_maximum_fusion.2), channel_id=1, source_target_pairs={{0,4},{2,6},{4,0},{6,2},{8,12},{10,14},{12,8},{14,10},{1,5},{3,7},... | collective-permute-start | bytes 393224 | tf_op jit(solution)/shard_map/ppermute | solution.py:237
  17.6 2.7 %collective-permute-start.3 = (bf16[16,32,128]{2,1,0:T(8,128)(2,1)S(1)}, bf16[16,32,128]{2,1,0:T(8,128)(2,1)S(1)}, u32[]{:S(2)}, u32[]{:S(2)}) collective-permute-start(bf16[16,32,128]{2,1,0:T(8,128)(2,1)S(1)} %pad_maximum_fusion.3), channel_id=1, source_target_pairs={{0,8},{2,10},{4,12},{6,14},{8,0},{10,2},{12,4},{14,6},{1,9},{3,11}... | collective-permute-start | bytes 393224 | tf_op jit(solution)/shard_map/ppermute | solution.py:237
  20.3 0.1 collective-permute-start.4
  20.4 2.2 %collective-permute-done.2 = bf16[16,32,128]{2,1,0:T(8,128)(2,1)S(1)} collective-permute-done((bf16[16,32,128]{2,1,0:T(8,128)(2,1)S(1)}, bf16[16,32,128]{2,1,0:T(8,128)(2,1)S(1)}, u32[]{:S(2)}, u32[]{:S(2)}) %collective-permute-start.2) | collective-permute-done | bytes 131104 | tf_op jit(solution)/shard_map/ppermute | solution.py:237
  22.6 7.7 %collective-permute-done.3 = bf16[16,32,128]{2,1,0:T(8,128)(2,1)S(1)} collective-permute-done((bf16[16,32,128]{2,1,0:T(8,128)(2,1)S(1)}, bf16[16,32,128]{2,1,0:T(8,128)(2,1)S(1)}, u32[]{:S(2)}, u32[]{:S(2)}) %collective-permute-start.3) | collective-permute-done | bytes 131104 | tf_op jit(solution)/shard_map/ppermute | solution.py:237
  30.4 0.0 copy-start.1
  30.4 0.3 left_arrange.1.refs_0_
  30.7 0.1 collective-permute-start.5
  30.8 0.5 copy-done.1
  31.3 2.8 %right_prep.1.refs_2_ = bf16[32,32,128]{2,1,0:T(8,128)(2,1)S(1)} custom-call(s32[16]{0:T(128)S(1)} %copy-done.2, f32[16,4]{1,0:T(8,128)S(1)} %pad_maximum_fusion.5.terms_ref, bf16[2,2,128,128]{3,2,1,0:T(8,128)(2,1)S(1)} %copy-done.1, bf16[16,192,128]{2,1,0:T(8,128)(2,1)S(1)} %bitcast.22, bf16[16,64,128]{2,1,0:T(8,128)(2,1)S(1)} %bitcast.24), custom_call_target="tpu_custom_call" | custom-call | flops 2000000000 | bytes 1000000 | tf_op jit(solution)/shard_map/right_prep/pallas_call | solution.py:248
  34.1 3.1 %collective-permute-start.10 = (bf16[32,32,128]{2,1,0:T(8,128)(2,1)S(1)}, bf16[32,32,128]{2,1,0:T(8,128)(2,1)S(1)}, u32[]{:S(2)}, u32[]{:S(2)}) collective-permute-start(bf16[32,32,128]{2,1,0:T(8,128)(2,1)S(1)} %right_prep.1.refs_2_), channel_id=1, source_target_pairs={{0,8},{2,10},{4,12},{6,14},{8,0},{10,2},{12,4},{14,6},{1,9},{3,11}... | collective-permute-start | bytes 786440 | tf_op jit(solution)/shard_map/ppermute | solution.py:237
  37.1 0.0 collective-permute-start.8
  37.2 12.2 %collective-permute-done.10.refs_6_ = bf16[32,32,128]{2,1,0:T(8,128)(2,1)S(1)} collective-permute-done((bf16[32,32,128]{2,1,0:T(8,128)(2,1)S(1)}, bf16[32,32,128]{2,1,0:T(8,128)(2,1)S(1)}, u32[]{:S(2)}, u32[]{:S(2)}) %collective-permute-start.10) | collective-permute-done | bytes 262176 | tf_op jit(solution)/shard_map/ppermute | solution.py:237
  49.4 1.5 %collective-permute-start.7 = (bf16[32,32,128]{2,1,0:T(8,128)(2,1)S(1)}, bf16[32,32,128]{2,1,0:T(8,128)(2,1)S(1)}, u32[]{:S(2)}, u32[]{:S(2)}) collective-permute-start(bf16[32,32,128]{2,1,0:T(8,128)(2,1)S(1)} %right_prep.1.refs_2_), channel_id=1, source_target_pairs={{0,2},{2,0},{4,6},{6,4},{8,10},{10,8},{12,14},{14,12},{1,3},{3,1},... | collective-permute-start | bytes 786440 | tf_op jit(solution)/shard_map/ppermute | solution.py:237
  50.9 0.5 collective-permute-start.11
  51.4 0.0 collective-permute-done.8.refs_4_
  51.4 1.5 %collective-permute-start.9 = (bf16[32,32,128]{2,1,0:T(8,128)(2,1)S(1)}, bf16[32,32,128]{2,1,0:T(8,128)(2,1)S(1)}, u32[]{:S(2)}, u32[]{:S(2)}) collective-permute-start(bf16[32,32,128]{2,1,0:T(8,128)(2,1)S(1)} %collective-permute-done.8.refs_4_), channel_id=1, source_target_pairs={{0,2},{2,0},{4,6},{6,4},{8,10},{10,8},{12,14},{14,12},{1,3},{3,1},... | collective-permute-start | bytes 786440 | tf_op jit(solution)/shard_map/ppermute | solution.py:237
  52.9 4.1 %collective-permute-done.12.refs_8_ = bf16[32,32,128]{2,1,0:T(8,128)(2,1)S(1)} collective-permute-done((bf16[32,32,128]{2,1,0:T(8,128)(2,1)S(1)}, bf16[32,32,128]{2,1,0:T(8,128)(2,1)S(1)}, u32[]{:S(2)}, u32[]{:S(2)}) %collective-permute-start.12) | collective-permute-done | bytes 262176 | tf_op jit(solution)/shard_map/ppermute | solution.py:237
  57.0 1.5 %collective-permute-start.13 = (bf16[32,32,128]{2,1,0:T(8,128)(2,1)S(1)}, bf16[32,32,128]{2,1,0:T(8,128)(2,1)S(1)}, u32[]{:S(2)}, u32[]{:S(2)}) collective-permute-start(bf16[32,32,128]{2,1,0:T(8,128)(2,1)S(1)} %collective-permute-done.12.refs_8_), channel_id=1, source_target_pairs={{0,2},{2,0},{4,6},{6,4},{8,10},{10,8},{12,14},{14,12},{1,3},{3,1},... | collective-permute-start | bytes 786440 | tf_op jit(solution)/shard_map/ppermute | solution.py:237
  58.5 0.1 collective-permute-done.7.refs_3_
  58.5 5.6 %collective-permute-done.11.refs_7_ = bf16[32,32,128]{2,1,0:T(8,128)(2,1)S(1)} collective-permute-done((bf16[32,32,128]{2,1,0:T(8,128)(2,1)S(1)}, bf16[32,32,128]{2,1,0:T(8,128)(2,1)S(1)}, u32[]{:S(2)}, u32[]{:S(2)}) %collective-permute-start.11) | collective-permute-done | bytes 262176 | tf_op jit(solution)/shard_map/ppermute | solution.py:237
  64.2 5.6 %collective-permute-done.9.refs_5_ = bf16[32,32,128]{2,1,0:T(8,128)(2,1)S(1)} collective-permute-done((bf16[32,32,128]{2,1,0:T(8,128)(2,1)S(1)}, bf16[32,32,128]{2,1,0:T(8,128)(2,1)S(1)}, u32[]{:S(2)}, u32[]{:S(2)}) %collective-permute-start.9) | collective-permute-done | bytes 262176 | tf_op jit(solution)/shard_map/ppermute | solution.py:237
  69.8 4.0 %collective-permute-done.13.refs_9_ = bf16[32,32,128]{2,1,0:T(8,128)(2,1)S(1)} collective-permute-done((bf16[32,32,128]{2,1,0:T(8,128)(2,1)S(1)}, bf16[32,32,128]{2,1,0:T(8,128)(2,1)S(1)}, u32[]{:S(2)}, u32[]{:S(2)}) %collective-permute-start.13) | collective-permute-done | bytes 262176 | tf_op jit(solution)/shard_map/ppermute | solution.py:237
  73.8 11.4 %contract.1 = bf16[2,2048,4096]{2,1,0:T(8,128)(2,1)} custom-call(bf16[2,1024,256]{2,1,0:T(8,128)(2,1)S(1)} %left_arrange.1.refs_0_, bf16[2,1024,256]{2,1,0:T(8,128)(2,1)S(1)} %collective-permute-done.5.refs_1_, bf16[32,32,128]{2,1,0:T(8,128)(2,1)S(1)} %right_prep.1.refs_2_, bf16[32,32,128]{2,1,0:T(8,128)(2,1)S(1)} %collective-permute-done.7.refs_3_, ...), custom_call_target="tpu_custom_call" | custom-call | flops 8999999488 | bytes 36000000 | tf_op jit(solution)/shard_map/contract/pallas_call | solution.py:297
  (22 shorter events, 0.2 us)
Async XLA Ops:
  0.0 2.6 %copy-start.5 = (f32[4,2,2,2]{0,3,2,1:T(2,128)S(1)}, f32[4,2,2,2]{0,3,2,1:T(2,128)}, u32[]{:S(2)}) copy-start(f32[4,2,2,2]{0,3,2,1:T(2,128)} %param.11) | copy-start | bytes 388
  0.0 2.6 %copy-start.4 = (f32[4,2,2,2]{0,3,2,1:T(2,128)S(1)}, f32[4,2,2,2]{0,3,2,1:T(2,128)}, u32[]{:S(2)}) copy-start(f32[4,2,2,2]{0,3,2,1:T(2,128)} %param.10) | copy-start | bytes 388
  0.0 2.6 %copy-start.2 = (s32[16]{0:T(128)S(1)}, s32[16]{0:T(128)}, u32[]{:S(2)}) copy-start(s32[16]{0:T(128)} %index_ref.3) | copy-start | bytes 196
  0.0 2.6 %copy-start = (bf16[2,2,128,128]{3,2,1,0:T(8,128)(2,1)S(1)}, bf16[2,2,128,128]{3,2,1,0:T(8,128)(2,1)}, u32[]{:S(2)}) copy-start(bf16[2,2,128,128]{3,2,1,0:T(8,128)(2,1)} %gates_ref.2) | copy-start | bytes 393220
  0.0 2.6 %collective-permute-start = (bf16[16,2,8192]{2,1,0:T(2,128)(2,1)}, bf16[16,2,8192]{2,1,0:T(2,128)(2,1)S(1)}, u32[]{:S(2)}, u32[]{:S(2)}) collective-permute-start(bf16[16,2,8192]{2,1,0:T(2,128)(2,1)} %param.7), channel_id=1, source_target_pairs={{0,1},{1,0},{2,3},{3,2},{4,5},{5,4},{6,7},{7,6},{8,9},{9,8},{10,11... | collective-permute-start | bytes 1572872 | tf_op jit(solution)/shard_map/ppermute | solution.py:234
  2.6 6.1 %copy-start.3 = (bf16[16,2,4096]{2,1,0:T(2,128)(2,1)S(1)}, bf16[16,2,4096]{2,1,0:T(2,128)(2,1)}, u32[]{:S(2)}) copy-start(bf16[16,2,4096]{2,1,0:T(2,128)(2,1)} %param.8) | copy-start | bytes 786436
  6.1 9.5 %collective-permute-start.1 = (bf16[32,32,128]{2,1,0:T(8,128)(2,1)S(1)}, bf16[32,32,128]{2,1,0:T(8,128)(2,1)S(1)}, u32[]{:S(2)}, u32[]{:S(2)}) collective-permute-start(bf16[32,32,128]{2,1,0:T(8,128)(2,1)S(1)} %pad_maximum_fusion.1), channel_id=1, source_target_pairs={{0,2},{2,0},{4,6},{6,4},{8,10},{10,8},{12,14},{14,12},{1,3},{3,1},... | collective-permute-start | bytes 786440 | tf_op jit(solution)/shard_map/ppermute | solution.py:237
  8.8 22.1 %collective-permute-start.6 = (bf16[16,2,4096]{2,1,0:T(2,128)(2,1)S(1)}, bf16[16,2,4096]{2,1,0:T(2,128)(2,1)S(1)}, u32[]{:S(2)}, u32[]{:S(2)}) collective-permute-start(bf16[16,2,4096]{2,1,0:T(2,128)(2,1)S(1)} %copy-done.3), channel_id=1, source_target_pairs={{0,1},{1,0},{2,3},{3,2},{4,5},{5,4},{6,7},{7,6},{8,9},{9,8},{10,11... | collective-permute-start | bytes 786440 | tf_op jit(solution)/shard_map/ppermute | solution.py:234
  15.7 6.9 %collective-permute-start.2 = (bf16[16,32,128]{2,1,0:T(8,128)(2,1)S(1)}, bf16[16,32,128]{2,1,0:T(8,128)(2,1)S(1)}, u32[]{:S(2)}, u32[]{:S(2)}) collective-permute-start(bf16[16,32,128]{2,1,0:T(8,128)(2,1)S(1)} %pad_maximum_fusion.2), channel_id=1, source_target_pairs={{0,4},{2,6},{4,0},{6,2},{8,12},{10,14},{12,8},{14,10},{1,5},{3,7},... | collective-permute-start | bytes 393224 | tf_op jit(solution)/shard_map/ppermute | solution.py:237
  17.6 12.7 %collective-permute-start.3 = (bf16[16,32,128]{2,1,0:T(8,128)(2,1)S(1)}, bf16[16,32,128]{2,1,0:T(8,128)(2,1)S(1)}, u32[]{:S(2)}, u32[]{:S(2)}) collective-permute-start(bf16[16,32,128]{2,1,0:T(8,128)(2,1)S(1)} %pad_maximum_fusion.3), channel_id=1, source_target_pairs={{0,8},{2,10},{4,12},{6,14},{8,0},{10,2},{12,4},{14,6},{1,9},{3,11}... | collective-permute-start | bytes 393224 | tf_op jit(solution)/shard_map/ppermute | solution.py:237
  20.3 10.1 %collective-permute-start.4 = (bf16[16,32,128]{2,1,0:T(8,128)(2,1)S(1)}, bf16[16,32,128]{2,1,0:T(8,128)(2,1)S(1)}, u32[]{:S(2)}, u32[]{:S(2)}) collective-permute-start(bf16[16,32,128]{2,1,0:T(8,128)(2,1)S(1)} %pad_maximum_fusion.4), channel_id=1, source_target_pairs={{0,12},{2,14},{4,8},{6,10},{8,4},{10,6},{12,0},{14,2},{1,13},{3,15... | collective-permute-start | bytes 393224 | tf_op jit(solution)/shard_map/ppermute | solution.py:237
  30.4 0.9 %copy-start.1 = (bf16[2,2,128,128]{3,2,1,0:T(8,128)(2,1)S(1)}, bf16[2,2,128,128]{3,2,1,0:T(8,128)(2,1)}, u32[]{:S(2)}) copy-start(bf16[2,2,128,128]{3,2,1,0:T(8,128)(2,1)} %gates_ref.3) | copy-start | bytes 393220
  30.7 43.1 %collective-permute-start.5 = (bf16[2,1024,256]{2,1,0:T(8,128)(2,1)S(1)}, bf16[2,1024,256]{2,1,0:T(8,128)(2,1)S(1)}, u32[]{:S(2)}, u32[]{:S(2)}) collective-permute-start(bf16[2,1024,256]{2,1,0:T(8,128)(2,1)S(1)} %left_arrange.1.refs_0_), channel_id=1, source_target_pairs={{0,1},{1,0},{2,3},{3,2},{4,5},{5,4},{6,7},{7,6},{8,9},{9,8},{10,11... | collective-permute-start | bytes 3145736 | tf_op jit(solution)/shard_map/ppermute | solution.py:234
  34.1 15.3 %collective-permute-start.10 = (bf16[32,32,128]{2,1,0:T(8,128)(2,1)S(1)}, bf16[32,32,128]{2,1,0:T(8,128)(2,1)S(1)}, u32[]{:S(2)}, u32[]{:S(2)}) collective-permute-start(bf16[32,32,128]{2,1,0:T(8,128)(2,1)S(1)} %right_prep.1.refs_2_), channel_id=1, source_target_pairs={{0,8},{2,10},{4,12},{6,14},{8,0},{10,2},{12,4},{14,6},{1,9},{3,11}... | collective-permute-start | bytes 786440 | tf_op jit(solution)/shard_map/ppermute | solution.py:237
  37.1 14.3 %collective-permute-start.8 = (bf16[32,32,128]{2,1,0:T(8,128)(2,1)S(1)}, bf16[32,32,128]{2,1,0:T(8,128)(2,1)S(1)}, u32[]{:S(2)}, u32[]{:S(2)}) collective-permute-start(bf16[32,32,128]{2,1,0:T(8,128)(2,1)S(1)} %right_prep.1.refs_2_), channel_id=1, source_target_pairs={{0,4},{2,6},{4,0},{6,2},{8,12},{10,14},{12,8},{14,10},{1,5},{3,7},... | collective-permute-start | bytes 786440 | tf_op jit(solution)/shard_map/ppermute | solution.py:237
  49.4 7.6 %collective-permute-start.12 = (bf16[32,32,128]{2,1,0:T(8,128)(2,1)S(1)}, bf16[32,32,128]{2,1,0:T(8,128)(2,1)S(1)}, u32[]{:S(2)}, u32[]{:S(2)}) collective-permute-start(bf16[32,32,128]{2,1,0:T(8,128)(2,1)S(1)} %collective-permute-done.10.refs_6_), channel_id=1, source_target_pairs={{0,4},{2,6},{4,0},{6,2},{8,12},{10,14},{12,8},{14,10},{1,5},{3,7},... | collective-permute-start | bytes 786440 | tf_op jit(solution)/shard_map/ppermute | solution.py:237
  49.4 9.2 %collective-permute-start.7 = (bf16[32,32,128]{2,1,0:T(8,128)(2,1)S(1)}, bf16[32,32,128]{2,1,0:T(8,128)(2,1)S(1)}, u32[]{:S(2)}, u32[]{:S(2)}) collective-permute-start(bf16[32,32,128]{2,1,0:T(8,128)(2,1)S(1)} %right_prep.1.refs_2_), channel_id=1, source_target_pairs={{0,2},{2,0},{4,6},{6,4},{8,10},{10,8},{12,14},{14,12},{1,3},{3,1},... | collective-permute-start | bytes 786440 | tf_op jit(solution)/shard_map/ppermute | solution.py:237
  50.9 13.3 %collective-permute-start.11 = (bf16[32,32,128]{2,1,0:T(8,128)(2,1)S(1)}, bf16[32,32,128]{2,1,0:T(8,128)(2,1)S(1)}, u32[]{:S(2)}, u32[]{:S(2)}) collective-permute-start(bf16[32,32,128]{2,1,0:T(8,128)(2,1)S(1)} %collective-permute-done.10.refs_6_), channel_id=1, source_target_pairs={{0,2},{2,0},{4,6},{6,4},{8,10},{10,8},{12,14},{14,12},{1,3},{3,1},... | collective-permute-start | bytes 786440 | tf_op jit(solution)/shard_map/ppermute | solution.py:237
  51.4 18.4 %collective-permute-start.9 = (bf16[32,32,128]{2,1,0:T(8,128)(2,1)S(1)}, bf16[32,32,128]{2,1,0:T(8,128)(2,1)S(1)}, u32[]{:S(2)}, u32[]{:S(2)}) collective-permute-start(bf16[32,32,128]{2,1,0:T(8,128)(2,1)S(1)} %collective-permute-done.8.refs_4_), channel_id=1, source_target_pairs={{0,2},{2,0},{4,6},{6,4},{8,10},{10,8},{12,14},{14,12},{1,3},{3,1},... | collective-permute-start | bytes 786440 | tf_op jit(solution)/shard_map/ppermute | solution.py:237
  57.0 16.9 %collective-permute-start.13 = (bf16[32,32,128]{2,1,0:T(8,128)(2,1)S(1)}, bf16[32,32,128]{2,1,0:T(8,128)(2,1)S(1)}, u32[]{:S(2)}, u32[]{:S(2)}) collective-permute-start(bf16[32,32,128]{2,1,0:T(8,128)(2,1)S(1)} %collective-permute-done.12.refs_8_), channel_id=1, source_target_pairs={{0,2},{2,0},{4,6},{6,4},{8,10},{10,8},{12,14},{14,12},{1,3},{3,1},... | collective-permute-start | bytes 786440 | tf_op jit(solution)/shard_map/ppermute | solution.py:237
